TPU v7x, 32 devices: a whole 2x2x4 slice. The times are simulated.
32 devices in a mesh: gx: 4 (over x, core), gy: 4 (over z), gz: 2 (over y).
Axes of the slice: x: 2, y: 2, z: 4, core: 2. Of those that a mesh axis runs over, the one named last changes fastest.
Arguments:
- density: float32 [32, 64, 256], P('gx', 'gy', 'gz'), may hold values from 0.1 to 10
- x_faces: float32 [2, 64, 256], P(None, 'gy', 'gz'), may hold values from -6 to 6
- y_faces: float32 [2, 32, 256], P(None, 'gx', 'gz'), may hold values from -6 to 6
- z_faces: float32 [2, 32, 64], P(None, 'gx', 'gy'), may hold values from -6 to 6
Outputs:
- solution_field: float32 [32, 64, 256], P('gx', 'gy', 'gz')
- residual: float32 [32, 64, 256], P('gx', 'gy', 'gz')
All inputs are finite; a program needn't handle non-finite values.
Results may differ from a plain program's by a relative error of at most 0.0003.
Values sent between devices are 32-bit elements; how exact they have to be, the bound alone decides.
A program may use at most 64 MiB of HBM per device.

v0:
```python
import functools

import jax
import jax.numpy as jnp
from jax import lax
from jax.experimental import pallas as pl
from jax.experimental.pallas import tpu as pltpu
from jax.sharding import PartitionSpec as P

W = 1.0 / 9.0
COUPLING = 0.5
MESH = pl.DeviceIdType.MESH
REACH = 7


def lane_of(shape):
    return lax.broadcasted_iota(jnp.int32, shape, len(shape) - 1)


def roll(x, shift, axis):
    return pltpu.roll(x, shift % x.shape[axis], axis)


def kernel(
    ns, bx, by, bz, kx, ky,
    den_in, xf_in, yf_in, zf_in, both,
    fld, ysrc, yrec, zsrc, zrec, tmp, prol, dsrc, dside, win, wside, sums,
    fsend, frecv, dsend, drecv, ssend, srecv,
    xyrec, pk, vfld, vpk, zfld, zpk, den, xf, yf, zf, isem,
):
    nx, ny, nz = ns
    gx, gy, gz = (lax.axis_index(a) for a in ("gx", "gy", "gz"))
    hx, hy, hz = bx // 2, by // 2, bz // 2
    me = (gx * ny + gy) * nz + gz
    total = nx * ny * nz
    f32 = jnp.float32

    loads = [
        pltpu.make_async_copy(a, b, isem.at[i])
        for i, (a, b) in enumerate(((den_in, den), (xf_in, xf), (yf_in, yf), (zf_in, zf)))
    ]
    for load in loads:
        load.start()

    fld[...] = jnp.zeros_like(fld)
    yrec[...] = jnp.zeros_like(yrec)
    zrec[...] = jnp.zeros_like(zrec)
    win[...] = jnp.zeros_like(win)
    wside[...] = jnp.zeros_like(wside)
    xyrec[...] = jnp.zeros_like(xyrec)
    pk[...] = jnp.zeros_like(pk)

    barrier = pltpu.get_barrier_semaphore()

    def coords(flat):
        return (flat // (ny * nz), lax.rem(flat // nz, ny), lax.rem(flat, nz))

    def greet(step, c):
        other = lax.rem(me + step, total)
        pl.semaphore_signal(barrier, inc=1, device_id=coords(other), device_id_type=MESH)
        return c

    lax.fori_loop(1, total, greet, 0)

    for load in loads:
        load.wait()

    lane = lane_of((by, bz))
    eye = lax.broadcasted_iota(jnp.int32, (by, by), 0) == lax.broadcasted_iota(jnp.int32, (by, by), 1)
    row = lax.broadcasted_iota(jnp.int32, (by, bz), 0)
    planes = []
    for p in range(bx):
        r = -COUPLING * den[p]
        if p == 0:
            r = r + jnp.where(gx == 0, xf[0], 0.0)
        if p == bx - 1:
            r = r + jnp.where(gx == nx - 1, xf[1], 0.0)
        r = r + jnp.where((row == 0) & (gy == 0), yf[0, p : p + 1, :], 0.0)
        r = r + jnp.where((row == by - 1) & (gy == ny - 1), yf[1, p : p + 1, :], 0.0)
        for side, (at, edge) in enumerate(((0, 0), (bz - 1, nz - 1))):
            col = jnp.sum(jnp.where(eye, zf[side, p : p + 1, :], 0.0), axis=1, keepdims=True)
            r = r + jnp.where((lane == at) & (gz == edge), col, 0.0)
        planes.append(r)
    r0 = jnp.stack(planes)

    lane8 = lane_of((8, bz))
    lanef = lane_of((by + 16, bz))
    halves = by // 8
    own = pl.ds(8, by)

    def exists(x, y, z):
        return (x >= 0) & (x < nx) & (y >= 0) & (y < ny) & (z >= 0) & (z < nz)

    def transfer(items, do):
        for (dx, dy, dz), src, dst, ss, rs in items:
            def copy(src=src, dst=dst, ss=ss, rs=rs, to=(gx + dx, gy + dy, gz + dz)):
                return pltpu.make_async_remote_copy(
                    src, dst, ss, rs, device_id=to, device_id_type=MESH
                )

            if do == "start":
                @pl.when(exists(gx + dx, gy + dy, gz + dz))
                def _():
                    copy().start()
            elif do == "sent":
                @pl.when(exists(gx + dx, gy + dy, gz + dz))
                def _():
                    copy().wait_send()
            else:
                @pl.when(exists(gx - dx, gy - dy, gz - dz))
                def _():
                    copy().wait_recv()

    def messages(c):
        f = fld.at[c]
        raw = [
            ((1, 0, 0), f.at[bx : bx + 2, own], f.at[0:2, own]),
            ((-1, 0, 0), f.at[2:4, own], f.at[bx + 2 : bx + 4, own]),
            ((0, 1, 0), ysrc.at[c, 1], yrec.at[c, 0]),
            ((0, -1, 0), ysrc.at[c, 0], yrec.at[c, 1]),
        ]
        for dz in (1, -1):
            src, side = zsrc.at[c, (dz + 1) // 2], (1 - dz) // 2
            raw.append(((0, 0, dz), src, zrec.at[c, side, 0]))
            raw.append(((1, 0, dz), src, zrec.at[c, side, 1]))
            raw.append(((-1, 0, dz), src, zrec.at[c, side, 2]))
            raw.append(((0, 1, dz), src, zrec.at[c, side, 3]))
            raw.append(((0, -1, dz), src, zrec.at[c, side, 4]))
        for dx in (1, -1):
            for dy in (1, -1):
                i = (1 - dx) + (1 - dy) // 2
                raw.append(((dx, dy, 0), ysrc.at[c, (dy + 1) // 2, 0], xyrec.at[c, i]))
        return [
            (o, src, dst, fsend.at[c, i], frecv.at[c, i])
            for i, (o, src, dst) in enumerate(raw)
            if abs(o[0]) < nx and abs(o[1]) < ny and abs(o[2]) < nz
        ]

    def exchange(c, value):
        fld[c, 2 : bx + 2, 8 : 8 + by, :] = value
        for p in range(bx):
            for d in (0, 1):
                ysrc[c, 0, d, p : p + 1, :] = value[p, d : d + 1, :]
                ysrc[c, 1, d, p : p + 1, :] = value[p, by - 1 - d : by - d, :]
        for side, at in ((0, 0), (1, bz - 2)):
            out = jnp.zeros((8, bz), f32)
            for h in range(halves):
                for p in range(bx):
                    to = 2 * (h * bx + p)
                    moved = roll(value[p, 8 * h : 8 * h + 8, :], to - at, 1)
                    out = jnp.where(lane8 // 2 == to // 2, moved, out)
            zsrc[c, side] = out
        items = messages(c)
        if c == 0:
            pl.semaphore_wait(barrier, total - 1)
        transfer(items, "start")
        transfer(items, "here")
        for p in range(bx):
            for d in (0, 1):
                fld[c, p + 2, 7 - d : 8 - d, :] = yrec[c, 0, d, p : p + 1, :]
                fld[c, p + 2, 8 + by + d : 9 + by + d, :] = yrec[c, 1, d, p : p + 1, :]
        for i in range(4):
            plane, p = ((1, bx - 1), (bx + 2, 0))[i // 2]
            at = (7, 8 + by)[i % 2]
            fld[c, plane, at : at + 1, :] = xyrec[c, i, p : p + 1, :]
        for side in (0, 1):
            t = [zrec[c, side, i] for i in range(5)]
            for h in range(halves):
                o = jnp.where((lane8 >= 4) & (lane8 < 4 + 2 * bx), roll(t[0], 4 - 2 * bx * h, 1), 0.0)
                o = jnp.where(lane8 // 2 == 1, roll(t[1], 2 - 2 * (bx * h + bx - 1), 1), o)
                o = jnp.where(lane8 // 2 == bx + 2, roll(t[2], 2 * (bx + 2) - 2 * bx * h, 1), o)
                pk[c, side, 8 + 8 * h : 16 + 8 * h, :] = o
            inner = (lane8 >= 4) & (lane8 < 4 + 2 * bx)
            before = jnp.where(inner, roll(t[3], 4 - 2 * bx * (halves - 1), 1), 0.0)
            after = jnp.where(inner, roll(t[4], 4, 1), 0.0)
            pk[c, side, 7:8, :] = before[7:8]
            pk[c, side, 8 + by : 9 + by, :] = after[0:1]

    def operate(ref, packed, i, a, b):
        c = ref[i, a:b, :]
        ln = lane_of(c.shape)
        s = ref[i - 1, a:b, :] + ref[i + 1, a:b, :]
        s = s + ref[i, a - 1 : b - 1, :] + ref[i, a + 1 : b + 1, :]
        s = s + jnp.where(ln == 0, packed[0, a:b, 2 * i + 1 : 2 * i + 2], roll(c, 1, 1))
        s = s + jnp.where(ln == bz - 1, packed[1, a:b, 2 * i : 2 * i + 1], roll(c, -1, 1))
        return 6.0 * c - s

    offsets = [
        (dx, dy, dz)
        for dx in range(-kx, kx + 1) for dy in range(-ky, ky + 1) for dz in (-1, 0, 1)
        if (dx, dy, dz) != (0, 0, 0) and abs(dx) < nx and abs(dy) < ny and abs(dz) < nz
    ]

    def gathered(c):
        items = []
        for dx, dy, dz in offsets:
            i = ((dx + kx) * (2 * ky + 1) + dy + ky) * 3 + dz + 1
            rows = pl.ds((ky - dy) * hy, hy)
            if dz == 0:
                n = hx // 2
                src, dst = dsrc.at[c], win.at[c, pl.ds((kx - dx) * n, n), rows]
            else:
                n = hx // 4
                side = (1 - dz) // 2
                src, dst = dside.at[c, 1 - side], wside.at[c, side, pl.ds((kx - dx) * n, n), rows]
            items.append(((dx, dy, dz), src, dst, dsend.at[c, i], drecv.at[c, i]))
        return items

    wx, wy = (2 * kx + 1) * hx, (2 * ky + 1) * hy
    ex = kx * hx
    ey = ky * hy
    q = bz // 4

    def dims(n0, n1, half):
        shape = (n1 - n0, wy, bz)
        x = lax.broadcasted_iota(jnp.int32, shape, 0) + n0
        y = lax.broadcasted_iota(jnp.int32, shape, 1)
        z = lax.broadcasted_iota(jnp.int32, shape, 2)
        x = x + (gx * hx - ex) // half
        y = y + gy * hy - ey
        z = z + gz * hz - q
        return (
            (x >= 0) & (x < nx * hx // half) & (y >= 0) & (y < ny * hy) & (z >= 0) & (z < nz * hz)
        )

    def beside(v, step):
        m = v[1:-1]
        s = v[:-2] + v[2:]
        s = s + roll(m, step, 1) + roll(m, -step, 1)
        return s + roll(m, step, 2) + roll(m, -step, 2)

    def twin(v, axis):
        even = lax.broadcasted_iota(jnp.int32, v.shape, axis) % 2 == 0
        return v + jnp.where(even, roll(v, -1, axis), roll(v, 1, axis))

    def coarse(c):
        a0, a1 = ex - REACH, ex + hx + REACH
        zi = lane_of((wy, bz))
        d = []
        for p in range(a0, a1):
            t, l, h = win[c, p // 2], wside[c, 0, p // 4], wside[c, 1, p // 4]
            t = roll(t, hz, 1) if p % 2 else t
            l = roll(l, -q * (p % 4), 1) if p % 4 else l
            h = roll(h, q + hz - q * (p % 4), 1) if p % 4 != 3 else h
            d.append(jnp.where(zi < q, l, jnp.where(zi < q + hz, t, h)))
        d = jnp.stack(d)
        v = W * d
        defect = d[1:-1] - (6.0 * v[1:-1] - beside(v, 1))
        n = defect.shape[0] // 2
        defect = defect.reshape(n, 2, wy, bz)
        r = 0.5 * twin(twin(defect[:, 0] + defect[:, 1], 1), 2)
        b0 = (a0 + 1) // 2
        m2 = dims(b0, b0 + n, 2)
        r = jnp.where(m2, r, 0.0)
        e = W * r
        e = jnp.where(m2[1:-1], e[1:-1] + W * (r[1:-1] - (6.0 * e[1:-1] - beside(e, 2))), 0.0)
        r = r[2:-2]
        e = jnp.where(m2[2:-2], e[1:-1] + W * (r - (6.0 * e[1:-1] - beside(e, 2))), 0.0)
        k0 = (b0 + 2) * 2 - a0
        spread = jnp.stack([e, e], axis=1).reshape(2 * e.shape[0], wy, bz)
        d = d[k0 : k0 + spread.shape[0]]
        v = W * d + spread
        out = v[1:-1] + W * (d[1:-1] - (6.0 * v[1:-1] - beside(v, 1)))
        p0 = (b0 + 2) * 2 + 1
        return jnp.where(dims(p0, p0 + out.shape[0], 1), out, 0.0), p0

    li = lax.broadcasted_iota(jnp.int32, (bz, bz), 0)
    lj = lax.broadcasted_iota(jnp.int32, (bz, bz), 1)
    shrink = jnp.where(li // 2 == (lj - q + hz) % hz, 0.5, 0.0).astype(f32)
    grow = jnp.where(li == q + lj // 2, 1.0, 0.0).astype(f32)

    def dot(x, m):
        out = None
        for _ in range(3):
            part = x.astype(jnp.bfloat16)
            x = x - part.astype(f32)
            y = jnp.dot(part, m.astype(jnp.bfloat16), preferred_element_type=f32)
            out = y if out is None else out + y
        return out

    def cycle_and_image(c, r):
        exchange(c, r)
        rref = fld.at[c]
        for j in range(hx):
            d = r[2 * j] + r[2 * j + 1]
            for i in (2 * j + 2, 2 * j + 3):
                d = d - W * operate(rref, pk.at[c], i, 8, 8 + by)
            tmp[j] = d
        half = tmp[:, pl.ds(0, hy, stride=2), :] + tmp[:, pl.ds(1, hy, stride=2), :]
        d1 = dot(half.reshape(hx * hy, bz), shrink).reshape(hx, hy, bz)
        li = lane_of((hy, bz))
        for j in range(hx // 2):
            t = jnp.where((li >= q) & (li < q + hz), d1[2 * j], d1[2 * j + 1])
            dsrc[c, j] = t
            win[c, ex // 2 + j, ey : ey + hy, :] = t
        for j in range(hx // 4):
            lo, hi = d1[4 * j], d1[4 * j]
            lo = roll(lo, q, 1)
            for m in range(1, 4):
                lo = jnp.where(li // q == m, roll(d1[4 * j + m], q * (m + 1), 1), lo)
                hi = jnp.where(li // q == m, roll(d1[4 * j + m], q * m, 1), hi)
            dside[c, 0, j] = lo
            dside[c, 1, j] = hi
        transfer(gathered(c), "start")
        transfer(gathered(c), "here")
        e1, p0 = coarse(c)
        e1 = e1[ex - 1 - p0 : ex + hx + 1 - p0, ey - 4 : ey + hy + 4]
        n = hy + 8
        prol[:, pl.ds(0, n, stride=2), :] = e1
        prol[:, pl.ds(1, n, stride=2), :] = e1
        for side, at in ((0, q - 1), (1, q + hz)):
            o = W * pk[c, side]
            for j in range(hx + 2):
                o = o + jnp.where(lanef // 4 == j, prol[j, :, at : at + 1], 0.0)
            vpk[side] = o
        fine = dot(prol[...].reshape((hx + 2) * 2 * n, bz), grow).reshape(hx + 2, 2 * n, bz)
        for i in range(bx + 4):
            vfld[i] = W * rref[i] + fine[i // 2]
        for i in range(1, bx + 3):
            a, b = 7, 9 + by
            z = vfld[i, a:b, :] + W * (rref[i, a:b, :] - operate(vfld, vpk, i, a, b))
            zrow = lax.broadcasted_iota(jnp.int32, z.shape, 0)
            inside = ((zrow > 0) | (gy > 0)) & ((zrow < by + 1) | (gy < ny - 1))
            if i == 1:
                inside = inside & (gx > 0)
            if i == bx + 2:
                inside = inside & (gx < nx - 1)
            zfld[i, a:b, :] = jnp.where(inside, z, 0.0)
        for side, at in ((0, 0), (1, bz - 1)):
            o = vpk[side]
            s = roll(o, 2, 1) + roll(o, -2, 1) + roll(o, 1, 0) + roll(o, -1, 0)
            s = s + roll(o, 1 - 2 * side, 1)
            for i in range(2, bx + 2):
                s = s + jnp.where(lanef == 2 * i + 1 - side, vfld[i, :, at : at + 1], 0.0)
            inside = gz < nz - 1 if side else gz > 0
            zpk[side] = jnp.where(inside, o + W * (pk[c, side] - (6.0 * o - s)), 0.0)
        z = zfld[2 : bx + 2, 8 : 8 + by, :]
        return z, jnp.stack([operate(zfld, zpk, i, 8, 8 + by) for i in range(2, bx + 2)])

    z0, w = cycle_and_image(0, r0)
    u, aw = cycle_and_image(1, w)

    pairs = ((r0, z0), (z0, w), (r0, u), (w, u), (u, aw), (z0, aw))
    l1 = lane_of((1, bz))
    mine = jnp.zeros((1, bz), f32)
    for i, (a, b) in enumerate(pairs):
        s = jnp.sum(jnp.sum(jnp.sum(a * b, axis=0), axis=0, keepdims=True), axis=1, keepdims=True)
        mine = jnp.where(l1 == i, s, mine)
    sums[me] = mine

    def share(do):
        def step(i, carry):
            other = lax.rem(me + i, total)
            source = lax.rem(me + total - i, total)
            if do == "start":
                pltpu.make_async_remote_copy(
                    sums.at[me], sums.at[me], ssend.at[i], srecv.at[i],
                    device_id=coords(other), device_id_type=MESH,
                ).start()
            else:
                pltpu.make_async_remote_copy(
                    sums.at[me], sums.at[source], ssend.at[i], srecv.at[i],
                    device_id=coords(other), device_id_type=MESH,
                ).wait()
            return carry

        lax.fori_loop(1, total, step, 0)

    share("start")
    for c in (0, 1):
        transfer(messages(c), "sent")
        transfer(gathered(c), "sent")
    share("wait")
    tot = jnp.sum(sums[...], axis=0)

    def scalar(i):
        return jnp.sum(jnp.where(l1 == i, tot, 0.0), axis=1, keepdims=True)

    g0, d0, ru, wu, uv, zv = (scalar(i) for i in range(6))
    a = g0 / d0
    g1 = (g0 - a * d0) - a * ru + a * a * wu
    beta = g1 / g0
    zaz = d0 - a * (wu + zv) + a * a * uv
    cross = (d0 - a * wu) + (d0 - a * zv)
    b = g1 / (zaz + beta * cross + beta * beta * d0)
    for p in range(bx):
        d1 = (z0[p] - a * u[p]) + beta * z0[p]
        i1 = (w[p] - a * aw[p]) + beta * w[p]
        both[0, p] = a * z0[p] + b * d1
        both[1, p] = (r0[p] - a * w[p]) - b * i1


def solution(mesh):
    ns = tuple(mesh.shape[a] for a in ("gx", "gy", "gz"))

    def local(density, x_faces, y_faces, z_faces):
        bx, by, bz = density.shape
        kx = min(-(-REACH // (bx // 2)), 10**6)
        ky = -(-REACH // (by // 2))
        hx, hy = bx // 2, by // 2
        vm = pl.BlockSpec(memory_space=pltpu.VMEM)
        total = ns[0] * ns[1] * ns[2]
        near = (2 * kx + 1) * (2 * ky + 1) * 3
        f32 = jnp.float32
        dma = pltpu.SemaphoreType.DMA
        both = pl.pallas_call(
            functools.partial(kernel, ns, bx, by, bz, kx, ky),
            out_shape=jax.ShapeDtypeStruct((2,) + density.shape, f32),
            in_specs=[pl.BlockSpec(memory_space=pl.ANY)] * 4,
            out_specs=vm,
            scratch_shapes=[
                pltpu.VMEM((2, bx + 4, by + 16, bz), f32),
                pltpu.VMEM((2, 2, 2, bx, bz), f32),
                pltpu.VMEM((2, 2, 2, bx, bz), f32),
                pltpu.VMEM((2, 2, 8, bz), f32),
                pltpu.VMEM((2, 2, 5, 8, bz), f32),
                pltpu.VMEM((hx, by, bz), f32),
                pltpu.VMEM((hx + 2, by + 16, bz), f32),
                pltpu.VMEM((2, hx // 2, hy, bz), f32),
                pltpu.VMEM((2, 2, hx // 4, hy, bz), f32),
                pltpu.VMEM((2, (2 * kx + 1) * hx // 2, (2 * ky + 1) * hy, bz), f32),
                pltpu.VMEM((2, 2, (2 * kx + 1) * hx // 4, (2 * ky + 1) * hy, bz), f32),
                pltpu.VMEM((total, 1, bz), f32),
                dma((2, 18)),
                dma((2, 18)),
                dma((2, near)),
                dma((2, near)),
                dma((total,)),
                dma((total,)),
                pltpu.VMEM((2, 4, bx, bz), f32),
                pltpu.VMEM((2, 2, by + 16, bz), f32),
                pltpu.VMEM((bx + 4, by + 16, bz), f32),
                pltpu.VMEM((2, by + 16, bz), f32),
                pltpu.VMEM((bx + 4, by + 16, bz), f32),
                pltpu.VMEM((2, by + 16, bz), f32),
                pltpu.VMEM(density.shape, f32),
                pltpu.VMEM(x_faces.shape, f32),
                pltpu.VMEM(y_faces.shape, f32),
                pltpu.VMEM(z_faces.shape, f32),
                dma((4,)),
            ],
            compiler_params=pltpu.CompilerParams(collective_id=0, has_side_effects=True),
        )(density, x_faces, y_faces, z_faces)
        return both[0], both[1]

    return jax.shard_map(
        local,
        mesh=mesh,
        in_specs=(P("gx", "gy", "gz"), P(None, "gy", "gz"), P(None, "gx", "gz"), P(None, "gx", "gy")),
        out_specs=(P("gx", "gy", "gz"), P("gx", "gy", "gz")),
        check_vma=False,
    )
```

profile of v0, /device:TPU:0, one launch (start us, length us, event | category | flops | bytes accessed | tf_op | source)
XLA Modules:
  0.0 35.2 jit_solution(3458707333177327932)
XLA Ops:
  0.6 33.0 %shard_map.59 = f32[2,8,16,128]{3,2,1,0:T(8,128)} custom-call(f32[8,16,128]{2,1,0:T(8,128)} %den_in.1, f32[2,16,128]{2,1,0:T(8,128)} %xf_in.1, f32[2,8,128]{2,1,0:T(8,128)} %yf_in.1, f32[2,8,16]{2,1,0:T(8,128)} %zf_in.1), custom_call_target="tpu_custom_call" | custom-call | tf_op jit(solution)/shard_map/pallas_call | solution.py:406
  33.6 1.5 %slice_bitcast_fusion = (f32[8,16,128]{2,1,0:T(8,128)}, f32[8,16,128]{2,1,0:T(8,128)}) fusion(f32[2,8,16,128]{3,2,1,0:T(8,128)} %shard_map.59), kind=kLoop, calls=%fused_computation | loop fusion | bytes 262144 | tf_op jit(solution)/shard_map/squeeze | solution.py:444
where the time goes:
time: 35.3 us; the launch traced here: 35.2 us
  Pallas kernels  33 us (93%)
  local copies, waits for them, and re-layouts  1.53 us (4%)
  between operations  0.64 us (2%)
    pallas_call x1, Pallas kernels, local(): pl.pallas_call(functools.partial(kernel, ns, bx, by, bz, kx, ky), out_sha...  33 us
    squeeze x1, local copies, waits for them, and re-layouts, local(): return (both[0], both[1])  1.53 us

commit v1 on v0

v1 whole, which is shorter than its diff:
```python
import functools
import itertools

import jax
import jax.numpy as jnp
from jax import lax
from jax.experimental import pallas as pl
from jax.experimental.pallas import tpu as pltpu
from jax.sharding import PartitionSpec as P

W = 1.0 / 9.0
COUPLING = 0.5
MESH = pl.DeviceIdType.MESH
REACH = 7
CUT = 8
CHUNK = 16
GROUPS = 64


def lane_of(shape):
    return lax.broadcasted_iota(jnp.int32, shape, len(shape) - 1)


def row_of(shape):
    return lax.broadcasted_iota(jnp.int32, shape, len(shape) - 2)


def roll(x, shift, axis):
    shift = shift % x.shape[axis]
    return pltpu.roll(x, shift, axis) if shift else x


def both_of(a, b):
    return b if a is None else a if b is None else a & b


def partners(g, n, reach):
    out = []
    for m in range(1, min(reach, n - 1) + 1):
        if n == 2:
            out.append((1 - 2 * g, None, None, 0, m))
        elif n == 4 and m == 1:
            inner = (g == 1) | (g == 2)
            out.append((1 - 2 * (g % 2), None, None, 0, m))
            out.append((3 - 2 * g, inner, inner, 1, m))
        elif n == 4 and m == 2:
            out.append((2 - 4 * (g // 2), None, None, 0, m))
        else:
            out.append((m, g + m < n, g - m >= 0, 2 * m - 1, m))
            out.append((-m, g - m >= 0, g + m < n, 2 * m, m))
    return out


def knows_all(ns, kx, ky):
    return ns[0] - 1 <= 3 * kx and ns[1] - 1 <= 3 * ky and ns[2] - 1 <= 3


def kernel(
    ns, bx, by, bz, kx, ky,
    den_in, xf_in, yf_in, zf_in, field_out, residual_out,
    fld, ysrc, yrec, zsrc, zrec, xyrec, pk,
    tu, tx, ty, shrink, grow, dsrc, dside, win, wside, prol, sums, blank,
    vfld, vpk, zfld, zpk, den, xf, yf, zf,
    fsend, frecv, dsend, drecv, ssend, srecv, isem,
):
    nx, ny, nz = ns
    gx, gy, gz = (lax.axis_index(a) for a in ("gx", "gy", "gz"))
    hx, hy, hz = bx // 2, by // 2, bz // 2
    q = bz // 4
    me = (gx * ny + gy) * nz + gz
    total = nx * ny * nz
    f32 = jnp.float32
    bf16 = jnp.bfloat16

    loads = [
        pltpu.make_async_copy(a, b, isem.at[i])
        for i, (a, b) in enumerate(((den_in, den), (xf_in, xf), (yf_in, yf), (zf_in, zf)))
    ]
    for load in loads:
        load.start()

    here = [(0, None, None, 0, 0)]
    window = []
    for o in itertools.product(here + partners(gx, nx, kx), here + partners(gy, ny, ky), here + partners(gz, nz, 1)):
        d, send, recv, key, far = zip(*o)
        if any(far):
            window.append((d, functools.reduce(both_of, send), functools.reduce(both_of, recv), key, far))
    window.sort(key=lambda item: -sum(f > 0 for f in item[4]))

    def at(d):
        return (gx + d[0], gy + d[1], gz + d[2])

    def only(cond, do):
        if cond is None:
            do()
        else:
            pl.when(cond)(do)

    def clear(c):
        for ref in (fld, yrec, zrec, xyrec, win, wside):
            ref[c] = jnp.zeros(ref.shape[1:], f32)

    clear(0)
    barrier = pltpu.get_barrier_semaphore()
    if knows_all(ns, kx, ky):
        callers = 0
        for d, send, recv, _, _ in window:
            only(send, lambda d=d: pl.semaphore_signal(barrier, inc=1, device_id=at(d), device_id_type=MESH))
            callers = callers + (1 if recv is None else jnp.where(recv, 1, 0))
    else:
        callers = total - 1

        def greet(step, c):
            o = lax.rem(me + step, total)
            to = (o // (ny * nz), lax.rem(o // nz, ny), lax.rem(o, nz))
            pl.semaphore_signal(barrier, inc=1, device_id=to, device_id_type=MESH)
            return c

        lax.fori_loop(1, total, greet, 0)

    clear(1)
    pk[...] = jnp.zeros_like(pk)
    tx[...] = jnp.zeros_like(tx)

    lj = lane_of((bz, bz))
    li = row_of((bz, bz))
    maps = (
        ((lj - q + hz) % hz, lj >= 0),
        (hz - CUT + lj % CHUNK, lj % CHUNK <= CUT),
        (lj % CHUNK - 1, lj % CHUNK <= CUT),
        (jnp.where(lj < q, -1, hz), (lj < q) | (lj >= q + hz)),
    )
    for i, (col, ok) in enumerate(maps):
        ok = ok & ((col >= 0) | (gz > 0)) & ((col < hz) | (gz < nz - 1))
        cell = (li // 2 == col) & ok
        outer = ((li == 2 * col - 1) | (li == 2 * col + 2)) & ok
        shrink[0:bz, i * bz : (i + 1) * bz] = jnp.where(cell, 0.5, 0.0).astype(bf16)
        shrink[bz : 2 * bz, i * bz : (i + 1) * bz] = jnp.where(outer, 0.5, 0.0).astype(bf16)
    grow[...] = jnp.where(li == q + lj // 2, 1.0, 0.0).astype(bf16)

    for load in loads:
        load.wait()

    lane = lane_of((by, bz))
    eye = row_of((by, by)) == lane_of((by, by))
    row = row_of((by, bz))
    planes = []
    for p in range(bx):
        r = -COUPLING * den[p]
        if p == 0:
            r = r + jnp.where(gx == 0, xf[0], 0.0)
        if p == bx - 1:
            r = r + jnp.where(gx == nx - 1, xf[1], 0.0)
        r = r + jnp.where((row == 0) & (gy == 0), yf[0, p : p + 1, :], 0.0)
        r = r + jnp.where((row == by - 1) & (gy == ny - 1), yf[1, p : p + 1, :], 0.0)
        for side, (a, edge) in enumerate(((0, 0), (bz - 1, nz - 1))):
            col = jnp.sum(jnp.where(eye, zf[side, p : p + 1, :], 0.0), axis=1, keepdims=True)
            r = r + jnp.where((lane == a) & (gz == edge), col, 0.0)
        planes.append(r)
    r0 = jnp.stack(planes)

    lane8 = lane_of((8, bz))
    lanef = lane_of((by + 16, bz))
    halves = by // 8
    own = pl.ds(8, by)

    def start(items, ssem, rsem):
        for d, send, _, key, _, src, dst in items:
            k = group(key)
            only(send, lambda d=d, src=src, dst=dst, k=k: pltpu.make_async_remote_copy(
                src, dst, ssem.at[k], rsem.at[k], device_id=at(d), device_id_type=MESH
            ).start())

    def group(key):
        return (key[0] * (2 * ky + 1) + key[1]) * 3 + key[2]

    def tiles(ref):
        n = 1
        for s in ref.shape:
            n *= s
        return n // (8 * bz)

    def arrive(items, sem, which):
        counts = {}
        for item in items:
            k = group(item[3])
            counts[k] = (counts.get(k, (0, None))[0] + tiles(item[6]), item[which])
        for k, (n, cond) in counts.items():
            room = blank.at[pl.ds(0, n)]
            only(cond, lambda room=room, k=k: pltpu.make_async_copy(room, room, sem.at[k]).wait())

    def halo(c):
        f = fld.at[c]
        out = []
        for d, send, recv, key, far in window:
            if max(far) > 1 or sum(far) > 2:
                continue
            dx, dy, dz = d
            if far == (1, 0, 0):
                src = f.at[pl.ds(2 + (bx - 2) * ((dx + 1) // 2), 2), own]
                dst = f.at[pl.ds((bx + 2) * ((1 - dx) // 2), 2), own]
            elif far == (0, 1, 0):
                src, dst = ysrc.at[c, (dy + 1) // 2], yrec.at[c, (1 - dy) // 2]
            elif far == (1, 1, 0):
                src, dst = ysrc.at[c, (dy + 1) // 2, 0], xyrec.at[c, (1 - dx) + (1 - dy) // 2]
            else:
                slot = 1 + (1 - dx) // 2 if far[0] else 3 + (1 - dy) // 2 if far[1] else 0
                src, dst = zsrc.at[c, (dz + 1) // 2], zrec.at[c, (1 - dz) // 2, slot]
            out.append((d, send, recv, key, far, src, dst))
        return out

    def gathered(c):
        out = []
        for d, send, recv, key, far in window:
            dx, dy, dz = d
            rows = pl.ds(pl.multiple_of((ky - dy) * hy, 8), hy)
            if far[2]:
                src, dst = dside.at[c, (dz + 1) // 2], wside.at[c, (1 - dz) // 2, kx - dx, rows]
            else:
                src, dst = dsrc.at[c], win.at[c, pl.ds((kx - dx) * 4, 4), rows]
            out.append((d, send, recv, key, far, src, dst))
        return out

    def split(x):
        parts = []
        for _ in range(3):
            part = x.astype(bf16)
            x = x - part.astype(f32)
            parts.append(part)
        return parts

    center = (lane8 >= q) & (lane8 < q + hz)

    def send_halo(c, value):
        fld[c, 2 : bx + 2, 8 : 8 + by, :] = value
        for p in range(bx):
            for d in (0, 1):
                ysrc[c, 0, d, p : p + 1, :] = value[p, d : d + 1, :]
                ysrc[c, 1, d, p : p + 1, :] = value[p, by - 1 - d : by - d, :]
        for side, a in ((0, 0), (1, bz - 2)):
            out = jnp.zeros((8, bz), f32)
            for h in range(halves):
                for p in range(bx):
                    to = 2 * (h * bx + p)
                    moved = roll(value[p, 8 * h : 8 * h + 8, :], to - a, 1)
                    out = jnp.where(lane8 // 2 == to // 2, moved, out)
            zsrc[c, side] = out

    def send_coarse(c, v):
        for i in range(hx):
            pair = v[2 * i] + v[2 * i + 1]
            ends = (v[2 * i - 1] if i else 0.0) + (v[2 * i + 2] if i < hx - 1 else 0.0)
            tu[i] = (1.0 - 3.0 * W) * pair + W * ends
            tx[i, 8 : 8 + by, :] = pair
            ty[i : i + 1, :] = jnp.where(gy > 0, W, 0.0) * pair[0:1]
            ty[hx + i : hx + i + 1, :] = jnp.where(gy < ny - 1, W, 0.0) * pair[by - 1 : by]
        tu[hx] = jnp.where(gx > 0, W, 0.0) * v[0]
        tu[hx + 1] = jnp.where(gx < nx - 1, W, 0.0) * v[bx - 1]

        def rows(ref, a):
            return ref[:, pl.ds(a, hy, stride=2), :]

        g = rows(tu, 0) + rows(tu, 1)
        outer = W * (rows(tx, 7) + rows(tx, 10))
        side = W * (rows(tx, 8) + rows(tx, 9))
        n = hx * hy
        left = jnp.concatenate(
            [(g[:hx] + outer).reshape(n, bz), g[hx:].reshape(2 * hy, bz), ty[...], jnp.zeros((8, bz), f32)]
        )
        right = jnp.concatenate([side.reshape(n, bz), jnp.zeros((2 * hy + 16, bz), f32)])
        m = left.shape[0]
        x = jnp.concatenate([left, right], axis=1)
        y = jnp.dot(jnp.concatenate(split(x)), shrink[...], preferred_element_type=f32)
        y = y[:m] + y[m : 2 * m] + y[2 * m :]

        def piece(i, k):
            return y[8 * i : 8 * i + 8, k * bz : (k + 1) * bz]

        for i in range(hx // 2 + 1):
            dsrc[c, i] = jnp.where(center, piece(2 * i, 0), piece(2 * i + 1, 0))
        skin = jnp.where(center, piece(hx + 2, 0), 0.0)
        for i in range(hx):
            skin = jnp.where((lane8 == q - 1 - 2 * i) | (lane8 == q + hz + 2 * i), piece(i, 3), skin)
        dsrc[c, hx // 2 + 1] = skin
        for s, k in ((1, 1), (0, 2)):
            out = jnp.zeros((8, bz), f32)
            for i in range(hx + 3):
                out = jnp.where(lane8 // CHUNK == i, piece(i, k), out)
            dside[c, s] = out
        for i in range(hx // 2 + 2):
            win[c, kx * 4 + i, ky * hy : (ky + 1) * hy, :] = dsrc[c, i]

    def place_halo(c):
        for p in range(bx):
            for d in (0, 1):
                fld[c, p + 2, 7 - d : 8 - d, :] = yrec[c, 0, d, p : p + 1, :]
                fld[c, p + 2, 8 + by + d : 9 + by + d, :] = yrec[c, 1, d, p : p + 1, :]
        for i in range(4):
            plane, p = ((1, bx - 1), (bx + 2, 0))[i // 2]
            a = (7, 8 + by)[i % 2]
            fld[c, plane, a : a + 1, :] = xyrec[c, i, p : p + 1, :]
        for side in (0, 1):
            t = [zrec[c, side, i] for i in range(5)]
            for h in range(halves):
                o = jnp.where((lane8 >= 4) & (lane8 < 4 + 2 * bx), roll(t[0], 4 - 2 * bx * h, 1), 0.0)
                o = jnp.where(lane8 // 2 == 1, roll(t[1], 2 - 2 * (bx * h + bx - 1), 1), o)
                o = jnp.where(lane8 // 2 == bx + 2, roll(t[2], 2 * (bx + 2) - 2 * bx * h, 1), o)
                pk[c, side, 8 + 8 * h : 16 + 8 * h, :] = o
            inner = (lane8 >= 4) & (lane8 < 4 + 2 * bx)
            before = jnp.where(inner, roll(t[3], 4 - 2 * bx * (halves - 1), 1), 0.0)
            after = jnp.where(inner, roll(t[4], 4, 1), 0.0)
            pk[c, side, 7:8, :] = before[7:8]
            pk[c, side, 8 + by : 9 + by, :] = after[0:1]

    def operate(ref, packed, i, a, b):
        c = ref[i, a:b, :]
        ln = lane_of(c.shape)
        s = ref[i - 1, a:b, :] + ref[i + 1, a:b, :]
        s = s + ref[i, a - 1 : b - 1, :] + ref[i, a + 1 : b + 1, :]
        s = s + jnp.where(ln == 0, packed[0, a:b, 2 * i + 1 : 2 * i + 2], roll(c, 1, 1))
        s = s + jnp.where(ln == bz - 1, packed[1, a:b, 2 * i : 2 * i + 1], roll(c, -1, 1))
        return 6.0 * c - s

    wy = (2 * ky + 1) * hy
    ex = kx * hx
    ey = ky * hy

    def dims(n0, n1, half):
        shape = (n1 - n0, wy, bz)
        x = lax.broadcasted_iota(jnp.int32, shape, 0) + n0
        y = lax.broadcasted_iota(jnp.int32, shape, 1)
        z = lax.broadcasted_iota(jnp.int32, shape, 2)
        x = x + (gx * hx - ex) // half
        y = y + gy * hy - ey
        z = z + gz * hz - q
        return (
            (x >= 0) & (x < nx * hx // half) & (y >= 0) & (y < ny * hy) & (z >= 0) & (z < nz * hz)
        )

    def beside(v, step):
        m = v[1:-1]
        s = v[:-2] + v[2:]
        s = s + roll(m, step, 1) + roll(m, -step, 1)
        return s + roll(m, step, 2) + roll(m, -step, 2)

    def twin(v, axis):
        even = lax.broadcasted_iota(jnp.int32, v.shape, axis) % 2 == 0
        return v + jnp.where(even, roll(v, -1, axis), roll(v, 1, axis))

    zi = lane_of((wy, bz))
    yi = row_of((wy, bz))
    mid = (zi >= q) & (zi < q + hz)
    low, high = (zi >= q - CUT) & (zi <= q), (zi >= q + hz - 1) & (zi < q + hz + CUT)

    def assemble(c, a0, a1):
        def spread(i, k):
            l = roll(wside[c, 0, i], q - CUT - CHUNK * k, 1)
            h = roll(wside[c, 1, i], q + hz - 1 - CHUNK * k, 1)
            return jnp.where(low, l, 0.0) + jnp.where(high, h, 0.0)

        def plane(i, k):
            t = roll(win[c, 4 * i + k // 2], hz * (k % 2), 1)
            return jnp.where(mid, t, 0.0) + spread(i, k)

        skins = [win[c, 4 * i + hx // 2 + 1] for i in range(2 * kx + 1)]
        ends = [jnp.where(mid, s, 0.0) + spread(i, hx + 2) for i, s in enumerate(skins)]
        d = []
        for p in range(a0, a1):
            i, k = p // hx, p % hx
            t = plane(i, k)
            if k == 0 and i > 0:
                t = t + plane(i - 1, hx + 1)
            if k == hx - 1 and i < 2 * kx:
                t = t + plane(i + 1, hx)
            t = t + jnp.where(yi % hy == hy - 1, roll(ends[i], -(k + 1), 0), 0.0)
            t = t + jnp.where(yi % hy == 0, roll(ends[i], hx - k, 0), 0.0)
            t = t + jnp.where(zi == q - 1, roll(skins[i], 2 * k, 1), 0.0)
            t = t + jnp.where(zi == q + hz, roll(skins[i], -2 * k, 1), 0.0)
            d.append(t)
        return jnp.stack(d)

    def coarse(c):
        a0, a1 = ex - REACH, ex + hx + REACH
        d = assemble(c, a0, a1)
        v = W * d
        defect = d[1:-1] - (6.0 * v[1:-1] - beside(v, 1))
        n = defect.shape[0] // 2
        defect = defect.reshape(n, 2, wy, bz)
        r = 0.5 * twin(twin(defect[:, 0] + defect[:, 1], 1), 2)
        b0 = (a0 + 1) // 2
        m2 = dims(b0, b0 + n, 2)
        r = jnp.where(m2, r, 0.0)
        e = W * r
        e = jnp.where(m2[1:-1], e[1:-1] + W * (r[1:-1] - (6.0 * e[1:-1] - beside(e, 2))), 0.0)
        r = r[2:-2]
        e = jnp.where(m2[2:-2], e[1:-1] + W * (r - (6.0 * e[1:-1] - beside(e, 2))), 0.0)
        k0 = (b0 + 2) * 2 - a0
        spread = jnp.stack([e, e], axis=1).reshape(2 * e.shape[0], wy, bz)
        d = d[k0 : k0 + spread.shape[0]]
        v = W * d + spread
        out = v[1:-1] + W * (d[1:-1] - (6.0 * v[1:-1] - beside(v, 1)))
        p0 = (b0 + 2) * 2 + 1
        return jnp.where(dims(p0, p0 + out.shape[0], 1), out, 0.0), p0

    def dot(x, m):
        out = None
        for part in split(x):
            y = jnp.dot(part, m, preferred_element_type=f32)
            out = y if out is None else out + y
        return out

    def cycle_and_image(c, r):
        send_halo(c, r)
        if c == 0:
            pl.semaphore_wait(barrier, callers)
        start(halo(c), fsend.at[c], frecv.at[c])
        send_coarse(c, r)
        start(gathered(c), dsend.at[c], drecv.at[c])
        arrive(halo(c), frecv.at[c], 2)
        place_halo(c)
        rref = fld.at[c]
        arrive(gathered(c), drecv.at[c], 2)
        e1, p0 = coarse(c)
        e1 = e1[ex - 1 - p0 : ex + hx + 1 - p0, ey - 4 : ey + hy + 4]
        n = hy + 8
        prol[:, pl.ds(0, n, stride=2), :] = e1
        prol[:, pl.ds(1, n, stride=2), :] = e1
        for side, a in ((0, q - 1), (1, q + hz)):
            o = W * pk[c, side]
            for j in range(hx + 2):
                o = o + jnp.where(lanef // 4 == j, prol[j, :, a : a + 1], 0.0)
            vpk[side] = o
        fine = dot(prol[...].reshape((hx + 2) * 2 * n, bz), grow[...]).reshape(hx + 2, 2 * n, bz)
        for i in range(bx + 4):
            vfld[i] = W * rref[i] + fine[i // 2]
        for i in range(1, bx + 3):
            a, b = 7, 9 + by
            z = vfld[i, a:b, :] + W * (rref[i, a:b, :] - operate(vfld, vpk, i, a, b))
            zrow = lax.broadcasted_iota(jnp.int32, z.shape, 0)
            inside = ((zrow > 0) | (gy > 0)) & ((zrow < by + 1) | (gy < ny - 1))
            if i == 1:
                inside = inside & (gx > 0)
            if i == bx + 2:
                inside = inside & (gx < nx - 1)
            zfld[i, a:b, :] = jnp.where(inside, z, 0.0)
        for side, a in ((0, 0), (1, bz - 1)):
            o = vpk[side]
            s = roll(o, 2, 1) + roll(o, -2, 1) + roll(o, 1, 0) + roll(o, -1, 0)
            s = s + roll(o, 1 - 2 * side, 1)
            for i in range(2, bx + 2):
                s = s + jnp.where(lanef == 2 * i + 1 - side, vfld[i, :, a : a + 1], 0.0)
            inside = gz < nz - 1 if side else gz > 0
            zpk[side] = jnp.where(inside, o + W * (pk[c, side] - (6.0 * o - s)), 0.0)
        z = zfld[2 : bx + 2, 8 : 8 + by, :]
        return z, jnp.stack([operate(zfld, zpk, i, 8, 8 + by) for i in range(2, bx + 2)])

    z0, w = cycle_and_image(0, r0)
    u, aw = cycle_and_image(1, w)

    pairs = ((r0, z0), (z0, w), (r0, u), (w, u), (u, aw), (z0, aw))
    l1 = lane_of((1, bz))
    mine = jnp.zeros((1, bz), f32)
    for i, (a, b) in enumerate(pairs):
        s = jnp.sum(jnp.sum(jnp.sum(a * b, axis=0), axis=0, keepdims=True), axis=1, keepdims=True)
        mine = jnp.where(l1 == i, s, mine)
    sums[me] = mine

    def share(to):
        pltpu.make_async_remote_copy(
            sums.at[me], sums.at[me], ssend.at[0], srecv.at[0], device_id=to, device_id_type=MESH
        ).start()

    if total <= GROUPS:
        ways = [[lax.rem(g + j, n) for j in range(n)] for g, n in zip((gx, gy, gz), ns)]
        for j in sorted(itertools.product(*(range(n) for n in ns)), key=lambda j: -sum(min(a, n - a) for a, n in zip(j, ns))):
            if any(j):
                share(tuple(way[a] for way, a in zip(ways, j)))
    else:

        def step(i, carry):
            o = lax.rem(me + i, total)
            share((o // (ny * nz), lax.rem(o // nz, ny), lax.rem(o, nz)))
            return carry

        lax.fori_loop(1, total, step, 0)

    rest = sums.at[pl.ds(0, total - 1)]
    pltpu.make_async_copy(rest, rest, srecv.at[0]).wait()
    tot = jnp.sum(sums[...], axis=0)

    def scalar(i):
        return jnp.sum(jnp.where(l1 == i, tot, 0.0), axis=1, keepdims=True)

    g0, d0, ru, wu, uv, zv = (scalar(i) for i in range(6))
    a = g0 / d0
    g1 = (g0 - a * d0) - a * ru + a * a * wu
    beta = g1 / g0
    zaz = d0 - a * (wu + zv) + a * a * uv
    cross = (d0 - a * wu) + (d0 - a * zv)
    b = g1 / (zaz + beta * cross + beta * beta * d0)
    for p in range(bx):
        d1 = (z0[p] - a * u[p]) + beta * z0[p]
        i1 = (w[p] - a * aw[p]) + beta * w[p]
        field_out[p] = a * z0[p] + b * d1
        residual_out[p] = (r0[p] - a * w[p]) - b * i1
    for c in (0, 1):
        arrive(halo(c), fsend.at[c], 1)
        arrive(gathered(c), dsend.at[c], 1)
    pltpu.make_async_copy(rest, rest, ssend.at[0]).wait()


def solution(mesh):
    ns = tuple(mesh.shape[a] for a in ("gx", "gy", "gz"))

    def local(density, x_faces, y_faces, z_faces):
        bx, by, bz = density.shape
        hx, hy = bx // 2, by // 2
        assert hx == 4 and hy == 8
        kx, ky = -(-REACH // hx), -(-REACH // hy)
        total = ns[0] * ns[1] * ns[2]
        f32 = jnp.float32
        dma = pltpu.SemaphoreType.DMA

        def vmem(*shape, dtype=f32):
            return pltpu.VMEM(shape, dtype)

        wy = (2 * ky + 1) * hy
        return pl.pallas_call(
            functools.partial(kernel, ns, bx, by, bz, kx, ky),
            out_shape=[vmem(bx, by, bz)] * 2,
            in_specs=[pl.BlockSpec(memory_space=pl.ANY)] * 4,
            out_specs=[pl.BlockSpec(memory_space=pltpu.VMEM)] * 2,
            scratch_shapes=[
                vmem(2, bx + 4, by + 16, bz),
                vmem(2, 2, 2, bx, bz),
                vmem(2, 2, 2, bx, bz),
                vmem(2, 2, 8, bz),
                vmem(2, 2, 5, 8, bz),
                vmem(2, 4, bx, bz),
                vmem(2, 2, by + 16, bz),
                vmem(hx + 2, by, bz),
                vmem(hx, by + 16, bz),
                vmem(2 * hx, bz),
                vmem(2 * bz, 4 * bz, dtype=jnp.bfloat16),
                vmem(bz, bz, dtype=jnp.bfloat16),
                vmem(2, 4, hy, bz),
                vmem(2, 2, hy, bz),
                vmem(2, (2 * kx + 1) * 4, wy, bz),
                vmem(2, 2, 2 * kx + 1, wy, bz),
                vmem(hx + 2, by + 16, bz),
                vmem(total, 1, bz),
                vmem(GROUPS, 8, bz),
                vmem(bx + 4, by + 16, bz),
                vmem(2, by + 16, bz),
                vmem(bx + 4, by + 16, bz),
                vmem(2, by + 16, bz),
                vmem(*density.shape),
                vmem(*x_faces.shape),
                vmem(*y_faces.shape),
                vmem(*z_faces.shape),
                dma((2, GROUPS)),
                dma((2, GROUPS)),
                dma((2, GROUPS)),
                dma((2, GROUPS)),
                dma((1,)),
                dma((1,)),
                dma((4,)),
            ],
            compiler_params=pltpu.CompilerParams(collective_id=0, has_side_effects=True),
        )(density, x_faces, y_faces, z_faces)

    return jax.shard_map(
        local,
        mesh=mesh,
        in_specs=(P("gx", "gy", "gz"), P(None, "gy", "gz"), P(None, "gx", "gz"), P(None, "gx", "gy")),
        out_specs=(P("gx", "gy", "gz"), P("gx", "gy", "gz")),
        check_vma=False,
    )
```

time: 35.3 us -> 28.9 us (0.82)
  Pallas kernels: 33 us -> 26.9 us
    pallas_call x1, Pallas kernels: 33 us -> 26.9 us  [local(): pl.pallas_call(functools.partial(kernel, ns, bx, by, bz, kx, ky), out_sha...]
    squeeze x1 -> x0, local copies, waits for them, and re-layouts: 1.53 us -> none  [local(): return (both[0], both[1])]
    unnamed x0 -> x2, local copies, waits for them, and re-layouts: none -> 1.26 us
where the time goes in v1:
time: 28.9 us; the launch traced here: 28.8 us
  Pallas kernels  26.9 us (93%)
  local copies, waits for them, and re-layouts  1.26 us (4%)
  between operations  0.64 us (2%)
    pallas_call x1, Pallas kernels, local(): pl.pallas_call(functools.partial(kernel, ns, bx, by, bz, kx, ky), out_sha...  26.9 us
    unnamed x2, local copies, waits for them, and re-layouts  1.26 us

profile of v1, /device:TPU:0, one launch (start us, length us, event | category | flops | bytes accessed | tf_op | source)
XLA Modules:
  0.0 28.8 jit_solution(4522457718250252557)
XLA Ops:
  0.6 26.9 %shard_map.59 = (f32[8,16,128]{2,1,0:T(8,128)S(1)}, f32[8,16,128]{2,1,0:T(8,128)S(1)}) custom-call(f32[8,16,128]{2,1,0:T(8,128)} %den_in.1, f32[2,16,128]{2,1,0:T(8,128)} %xf_in.1, f32[2,8,128]{2,1,0:T(8,128)} %yf_in.1, f32[2,8,16]{2,1,0:T(8,128)} %zf_in.1), custom_call_target="tpu_custom_call" | custom-call | tf_op jit(solution)/shard_map/pallas_call | solution.py:528
  27.5 0.6 %copy.8 = f32[8,16,128]{2,1,0:T(8,128)} copy(f32[8,16,128]{2,1,0:T(8,128)S(1)} %get-tuple-element.2) | data formatting | bytes 131072
  28.2 0.6 %copy.9 = f32[8,16,128]{2,1,0:T(8,128)} copy(f32[8,16,128]{2,1,0:T(8,128)S(1)} %get-tuple-element.3) | data formatting | bytes 131072

commit v2 on v1

--- a/solution.py
+++ b/solution.py
@@ -14,7 +14,7 @@
 REACH = 7
 CUT = 8
 CHUNK = 16
-GROUPS = 64
+ROWS = 2048
 
 
 def lane_of(shape):
@@ -61,7 +61,7 @@
     fld, ysrc, yrec, zsrc, zrec, xyrec, pk,
     tu, tx, ty, shrink, grow, dsrc, dside, win, wside, prol, sums, blank,
     vfld, vpk, zfld, zpk, den, xf, yf, zf,
-    fsend, frecv, dsend, drecv, ssend, srecv, isem,
+    ssem, rsem, isem,
 ):
     nx, ny, nz = ns
     gx, gy, gz = (lax.axis_index(a) for a in ("gx", "gy", "gz"))
@@ -74,7 +74,7 @@
 
     loads = [
         pltpu.make_async_copy(a, b, isem.at[i])
-        for i, (a, b) in enumerate(((den_in, den), (xf_in, xf), (yf_in, yf), (zf_in, zf)))
+        for i, a, b in ((0, den_in, den), (0, xf_in, xf), (0, yf_in, yf), (1, zf_in, zf))
     ]
     for load in loads:
         load.start()
@@ -101,6 +101,19 @@
             ref[c] = jnp.zeros(ref.shape[1:], f32)
 
     clear(0)
+    paired = all(n in (1, 2, 4) for n in ns)
+    inner = [(g == 1) | (g == 2) for g in (gx, gy, gz)]
+
+    def rows_of(ref):
+        n = 1
+        for size in ref.shape:
+            n *= size
+        return n // bz
+
+    def wait_rows(n, sem):
+        room = blank.at[pl.ds(0, n)]
+        pltpu.make_async_copy(room, room, sem).wait()
+
     barrier = pltpu.get_barrier_semaphore()
     if knows_all(ns, kx, ky):
         callers = 0
@@ -138,8 +151,8 @@
         shrink[bz : 2 * bz, i * bz : (i + 1) * bz] = jnp.where(outer, 0.5, 0.0).astype(bf16)
     grow[...] = jnp.where(li == q + lj // 2, 1.0, 0.0).astype(bf16)
 
-    for load in loads:
-        load.wait()
+    wait_rows(sum(rows_of(a) for a in (den, xf, yf)), isem.at[0])
+    loads[-1].wait()
 
     lane = lane_of((by, bz))
     eye = row_of((by, by)) == lane_of((by, by))
@@ -164,30 +177,29 @@
     halves = by // 8
     own = pl.ds(8, by)
 
-    def start(items, ssem, rsem):
-        for d, send, _, key, _, src, dst in items:
-            k = group(key)
-            only(send, lambda d=d, src=src, dst=dst, k=k: pltpu.make_async_remote_copy(
-                src, dst, ssem.at[k], rsem.at[k], device_id=at(d), device_id_type=MESH
+    def start(items, sem):
+        for d, send, _, _, _, src, dst in items:
+            only(send, lambda d=d, src=src, dst=dst: pltpu.make_async_remote_copy(
+                src, dst, ssem.at[0], sem, device_id=at(d), device_id_type=MESH
             ).start())
 
-    def group(key):
-        return (key[0] * (2 * ky + 1) + key[1]) * 3 + key[2]
-
-    def tiles(ref):
-        n = 1
-        for s in ref.shape:
-            n *= s
-        return n // (8 * bz)
-
-    def arrive(items, sem, which):
+    def arrive(items, sem, which, more=0):
         counts = {}
         for item in items:
-            k = group(item[3])
-            counts[k] = (counts.get(k, (0, None))[0] + tiles(item[6]), item[which])
-        for k, (n, cond) in counts.items():
-            room = blank.at[pl.ds(0, n)]
-            only(cond, lambda room=room, k=k: pltpu.make_async_copy(room, room, sem.at[k]).wait())
+            counts[item[3]] = (counts.get(item[3], (0,))[0] + rows_of(item[5]), item[which])
+        if not paired:
+            for n, cond in counts.values():
+                only(cond, lambda n=n: wait_rows(n, sem))
+            if more:
+                wait_rows(more, sem)
+            return
+        axes = [i for i in range(3) if ns[i] == 4 and any(key[i] for key in counts)]
+        for flags in itertools.product((0, 1), repeat=len(axes)):
+            state, cond = dict(zip(axes, flags)), None
+            for i, flag in state.items():
+                cond = both_of(cond, inner[i] if flag else jnp.logical_not(inner[i]))
+            n = sum(rows for key, (rows, _) in counts.items() if all(key[i] <= state.get(i, 0) for i in range(3)))
+            only(cond, lambda n=n: wait_rows(n + more, sem))
 
     def halo(c):
         f = fld.at[c]
@@ -413,13 +425,13 @@
         send_halo(c, r)
         if c == 0:
             pl.semaphore_wait(barrier, callers)
-        start(halo(c), fsend.at[c], frecv.at[c])
+        start(halo(c), rsem.at[2 * c])
         send_coarse(c, r)
-        start(gathered(c), dsend.at[c], drecv.at[c])
-        arrive(halo(c), frecv.at[c], 2)
+        start(gathered(c), rsem.at[2 * c + 1])
+        arrive(halo(c), rsem.at[2 * c], 2)
         place_halo(c)
         rref = fld.at[c]
-        arrive(gathered(c), drecv.at[c], 2)
+        arrive(gathered(c), rsem.at[2 * c + 1], 2)
         e1, p0 = coarse(c)
         e1 = e1[ex - 1 - p0 : ex + hx + 1 - p0, ey - 4 : ey + hy + 4]
         n = hy + 8
@@ -467,10 +479,10 @@
 
     def share(to):
         pltpu.make_async_remote_copy(
-            sums.at[me], sums.at[me], ssend.at[0], srecv.at[0], device_id=to, device_id_type=MESH
+            sums.at[me], sums.at[me], ssem.at[0], rsem.at[4], device_id=to, device_id_type=MESH
         ).start()
 
-    if total <= GROUPS:
+    if total <= 64:
         ways = [[lax.rem(g + j, n) for j in range(n)] for g, n in zip((gx, gy, gz), ns)]
         for j in sorted(itertools.product(*(range(n) for n in ns)), key=lambda j: -sum(min(a, n - a) for a, n in zip(j, ns))):
             if any(j):
@@ -484,8 +496,7 @@
 
         lax.fori_loop(1, total, step, 0)
 
-    rest = sums.at[pl.ds(0, total - 1)]
-    pltpu.make_async_copy(rest, rest, srecv.at[0]).wait()
+    wait_rows(total - 1, rsem.at[4])
     tot = jnp.sum(sums[...], axis=0)
 
     def scalar(i):
@@ -503,10 +514,7 @@
         i1 = (w[p] - a * aw[p]) + beta * w[p]
         field_out[p] = a * z0[p] + b * d1
         residual_out[p] = (r0[p] - a * w[p]) - b * i1
-    for c in (0, 1):
-        arrive(halo(c), fsend.at[c], 1)
-        arrive(gathered(c), dsend.at[c], 1)
-    pltpu.make_async_copy(rest, rest, ssend.at[0]).wait()
+    arrive([item for c in (0, 1) for item in halo(c) + gathered(c)], ssem.at[0], 1, total - 1)
 
 
 def solution(mesh):
@@ -549,7 +557,7 @@
                 vmem(2, 2, 2 * kx + 1, wy, bz),
                 vmem(hx + 2, by + 16, bz),
                 vmem(total, 1, bz),
-                vmem(GROUPS, 8, bz),
+                vmem(ROWS, 1, bz),
                 vmem(bx + 4, by + 16, bz),
                 vmem(2, by + 16, bz),
                 vmem(bx + 4, by + 16, bz),
@@ -558,13 +566,9 @@
                 vmem(*x_faces.shape),
                 vmem(*y_faces.shape),
                 vmem(*z_faces.shape),
-                dma((2, GROUPS)),
-                dma((2, GROUPS)),
-                dma((2, GROUPS)),
-                dma((2, GROUPS)),
                 dma((1,)),
-                dma((1,)),
-                dma((4,)),
+                dma((5,)),
+                dma((2,)),
             ],
             compiler_params=pltpu.CompilerParams(collective_id=0, has_side_effects=True),
         )(density, x_faces, y_faces, z_faces)

time: 28.9 us -> 24.4 us (0.84)
  Pallas kernels: 26.9 us -> 22.3 us
    pallas_call x1, Pallas kernels: 26.9 us -> 22.3 us  [local(): pl.pallas_call(functools.partial(kernel, ns, bx, by, bz, kx, ky), out_sha...]
where the time goes in v2:
time: 24.4 us; the launch traced here: 24.2 us
  Pallas kernels  22.3 us (91%)
  local copies, waits for them, and re-layouts  1.26 us (5%)
  between operations  0.64 us (3%)
    pallas_call x1, Pallas kernels, local(): pl.pallas_call(functools.partial(kernel, ns, bx, by, bz, kx, ky), out_sha...  22.3 us
    unnamed x2, local copies, waits for them, and re-layouts  1.26 us

profile of v2, /device:TPU:0, one launch (start us, length us, event | category | flops | bytes accessed | tf_op | source)
XLA Modules:
  0.0 24.2 jit_solution(7633653120690767436)
XLA Ops:
  0.6 22.3 %shard_map.59 = (f32[8,16,128]{2,1,0:T(8,128)S(1)}, f32[8,16,128]{2,1,0:T(8,128)S(1)}) custom-call(f32[8,16,128]{2,1,0:T(8,128)} %den_in.1, f32[2,16,128]{2,1,0:T(8,128)} %xf_in.1, f32[2,8,128]{2,1,0:T(8,128)} %yf_in.1, f32[2,8,16]{2,1,0:T(8,128)} %zf_in.1), custom_call_target="tpu_custom_call" | custom-call | tf_op jit(solution)/shard_map/pallas_call | solution.py:536
  22.9 0.6 %copy.8 = f32[8,16,128]{2,1,0:T(8,128)} copy(f32[8,16,128]{2,1,0:T(8,128)S(1)} %get-tuple-element.2) | data formatting | bytes 131072
  23.6 0.6 %copy.9 = f32[8,16,128]{2,1,0:T(8,128)} copy(f32[8,16,128]{2,1,0:T(8,128)S(1)} %get-tuple-element.3) | data formatting | bytes 131072

commit v3 on v2

--- a/solution.py
+++ b/solution.py
@@ -57,10 +57,10 @@
 
 def kernel(
     ns, bx, by, bz, kx, ky,
-    den_in, xf_in, yf_in, zf_in, field_out, residual_out,
+    den_in, xf_in, yf_in, zf_in, both,
     fld, ysrc, yrec, zsrc, zrec, xyrec, pk,
     tu, tx, ty, shrink, grow, dsrc, dside, win, wside, prol, sums, blank,
-    vfld, vpk, zfld, zpk, den, xf, yf, zf,
+    wedge, wd, pair, wb, wr, we, wv, vfld, vpk, zfld, zpk, den, xf, yf, zf,
     ssem, rsem, isem,
 ):
     nx, ny, nz = ns
@@ -134,6 +134,10 @@
     clear(1)
     pk[...] = jnp.zeros_like(pk)
     tx[...] = jnp.zeros_like(tx)
+    for ref in (wedge, wd, pair, wb, wr, we, wv):
+        rim = jnp.zeros((ref.shape[0], 8, bz), f32)
+        ref[:, 0:8, :] = rim
+        ref[:, ref.shape[1] - 8 :, :] = rim
 
     lj = lane_of((bz, bz))
     li = row_of((bz, bz))
@@ -324,95 +328,124 @@
             pk[c, side, 7:8, :] = before[7:8]
             pk[c, side, 8 + by : 9 + by, :] = after[0:1]
 
-    def operate(ref, packed, i, a, b):
+    def around(ref, packed, i, a, b):
         c = ref[i, a:b, :]
         ln = lane_of(c.shape)
         s = ref[i - 1, a:b, :] + ref[i + 1, a:b, :]
         s = s + ref[i, a - 1 : b - 1, :] + ref[i, a + 1 : b + 1, :]
         s = s + jnp.where(ln == 0, packed[0, a:b, 2 * i + 1 : 2 * i + 2], roll(c, 1, 1))
-        s = s + jnp.where(ln == bz - 1, packed[1, a:b, 2 * i : 2 * i + 1], roll(c, -1, 1))
-        return 6.0 * c - s
+        return s + jnp.where(ln == bz - 1, packed[1, a:b, 2 * i : 2 * i + 1], roll(c, -1, 1))
 
     wy = (2 * ky + 1) * hy
     ex = kx * hx
     ey = ky * hy
 
-    def dims(n0, n1, half):
-        shape = (n1 - n0, wy, bz)
-        x = lax.broadcasted_iota(jnp.int32, shape, 0) + n0
-        y = lax.broadcasted_iota(jnp.int32, shape, 1)
-        z = lax.broadcasted_iota(jnp.int32, shape, 2)
-        x = x + (gx * hx - ex) // half
-        y = y + gy * hy - ey
-        z = z + gz * hz - q
-        return (
-            (x >= 0) & (x < nx * hx // half) & (y >= 0) & (y < ny * hy) & (z >= 0) & (z < nz * hz)
-        )
-
-    def beside(v, step):
-        m = v[1:-1]
-        s = v[:-2] + v[2:]
-        s = s + roll(m, step, 1) + roll(m, -step, 1)
-        return s + roll(m, step, 2) + roll(m, -step, 2)
-
-    def twin(v, axis):
-        even = lax.broadcasted_iota(jnp.int32, v.shape, axis) % 2 == 0
-        return v + jnp.where(even, roll(v, -1, axis), roll(v, 1, axis))
-
-    zi = lane_of((wy, bz))
-    yi = row_of((wy, bz))
+    zi = lane_of((8, bz))
+    yi = row_of((8, bz))
     mid = (zi >= q) & (zi < q + hz)
     low, high = (zi >= q - CUT) & (zi <= q), (zi >= q + hz - 1) & (zi < q + hz + CUT)
+    if nz == 2:
+        sides = [(1 - gz, jnp.where(gz == 0, q + hz - 1, q - CUT), (high & (gz == 0)) | (low & (gz == 1)))]
+    else:
+        sides = [(0, q - CUT, low), (1, q + hz - 1, high)] if nz > 1 else []
+    strips = [slice(8 + 8 * t, 16 + 8 * t) for t in range(wy // 8)]
+
+    def grid_strip(t):
+        y = yi + 8 * t
+        ok = (y >= ey - gy * hy) & (y < ey + (ny - gy) * hy) & (zi >= q - gz * hz) & (zi < q + (nz - gz) * hz)
+        return jnp.where(ok, 1.0, 0.0)
+
+    def there(p, half):
+        x = p + (gx * hx - ex) // half
+        return jnp.where((x >= 0) & (x < nx * hx // half), 1.0, 0.0)
+
+    def total_of(terms):
+        while len(terms) > 1:
+            terms = [a + b for a, b in zip(terms[::2], terms[1::2])] + ([terms[-1]] if len(terms) % 2 else [])
+        return terms[0]
+
+    def shifted(ref, p, t, step):
+        v = ref[p, strips[t], :]
+        r0 = strips[t].start
+        return total_of([
+            ref[p, r0 - step : r0 - step + 8, :], ref[p, r0 + step : r0 + step + 8, :],
+            roll(v, step, 1), roll(v, -step, 1),
+        ])
 
     def assemble(c, a0, a1):
-        def spread(i, k):
-            l = roll(wside[c, 0, i], q - CUT - CHUNK * k, 1)
-            h = roll(wside[c, 1, i], q + hz - 1 - CHUNK * k, 1)
-            return jnp.where(low, l, 0.0) + jnp.where(high, h, 0.0)
-
-        def plane(i, k):
-            t = roll(win[c, 4 * i + k // 2], hz * (k % 2), 1)
-            return jnp.where(mid, t, 0.0) + spread(i, k)
-
-        skins = [win[c, 4 * i + hx // 2 + 1] for i in range(2 * kx + 1)]
-        ends = [jnp.where(mid, s, 0.0) + spread(i, hx + 2) for i, s in enumerate(skins)]
-        d = []
-        for p in range(a0, a1):
-            i, k = p // hx, p % hx
-            t = plane(i, k)
-            if k == 0 and i > 0:
-                t = t + plane(i - 1, hx + 1)
-            if k == hx - 1 and i < 2 * kx:
-                t = t + plane(i + 1, hx)
-            t = t + jnp.where(yi % hy == hy - 1, roll(ends[i], -(k + 1), 0), 0.0)
-            t = t + jnp.where(yi % hy == 0, roll(ends[i], hx - k, 0), 0.0)
-            t = t + jnp.where(zi == q - 1, roll(skins[i], 2 * k, 1), 0.0)
-            t = t + jnp.where(zi == q + hz, roll(skins[i], -2 * k, 1), 0.0)
-            d.append(t)
-        return jnp.stack(d)
+        def side_of(i, k, rows):
+            return [
+                (m, pltpu.roll(wside[c, s, i, rows, :], (base - CHUNK * k) % bz, 1)) for s, base, m in sides
+            ]
+
+        for t, strip in enumerate(strips):
+            rows = slice(8 * t, 8 * t + 8)
+            for i in range(2 * kx + 1):
+                e = jnp.where(mid, win[c, 4 * i + hx // 2 + 1, rows, :], 0.0)
+                for m, v in side_of(i, hx + 2, rows):
+                    e = e + jnp.where(m, v, 0.0)
+                wedge[i, strip, :] = e
+        for t, strip in enumerate(strips):
+            rows = slice(8 * t, 8 * t + 8)
+            for p in range(a0, a1):
+                i, k = p // hx, p % hx
+                parts = [(i, k)]
+                if k == 0 and i > 0:
+                    parts.append((i - 1, hx + 1))
+                if k == hx - 1 and i < 2 * kx:
+                    parts.append((i + 1, hx))
+                inner_part = total_of([roll(win[c, 4 * j + f // 2, rows, :], hz * (f % 2), 1) for j, f in parts])
+                terms = [jnp.where(mid, inner_part, 0.0)]
+                found = [side_of(j, f, rows) for j, f in parts]
+                for n, (_, _, m) in enumerate(sides):
+                    terms.append(jnp.where(m, total_of([f[n][1] for f in found]), 0.0))
+                up = 8 + 8 * t + k + 1
+                down = 8 + 8 * t - hx + k
+                terms.append(jnp.where(yi == 7, wedge[i, up : up + 8, :], jnp.where(yi == 0, wedge[i, down : down + 8, :], 0.0)))
+                skin = win[c, 4 * i + hx // 2 + 1, rows, :]
+                terms.append(jnp.where(zi == q - 1, roll(skin, 2 * k, 1), jnp.where(zi == q + hz, roll(skin, -2 * k, 1), 0.0)))
+                wd[p - a0, strip, :] = total_of(terms)
 
     def coarse(c):
         a0, a1 = ex - REACH, ex + hx + REACH
-        d = assemble(c, a0, a1)
-        v = W * d
-        defect = d[1:-1] - (6.0 * v[1:-1] - beside(v, 1))
-        n = defect.shape[0] // 2
-        defect = defect.reshape(n, 2, wy, bz)
-        r = 0.5 * twin(twin(defect[:, 0] + defect[:, 1], 1), 2)
+        assemble(c, a0, a1)
+        n = (a1 - a0) // 2 - 1
         b0 = (a0 + 1) // 2
-        m2 = dims(b0, b0 + n, 2)
-        r = jnp.where(m2, r, 0.0)
-        e = W * r
-        e = jnp.where(m2[1:-1], e[1:-1] + W * (r[1:-1] - (6.0 * e[1:-1] - beside(e, 2))), 0.0)
-        r = r[2:-2]
-        e = jnp.where(m2[2:-2], e[1:-1] + W * (r - (6.0 * e[1:-1] - beside(e, 2))), 0.0)
+        on2 = [there(b0 + j, 2) for j in range(n)]
+        grid = [grid_strip(t) for t in range(len(strips))]
+        every = list(enumerate(strips))
+        for t, strip in every:
+            for j in range(n):
+                pair[j, strip, :] = wd[2 * j + 1, strip, :] + wd[2 * j + 2, strip, :]
+        for t, strip in every:
+            for j in range(n):
+                ends = wd[2 * j, strip, :] + wd[2 * j + 3, strip, :]
+                wb[j, strip, :] = (1.0 - 5.0 * W) * pair[j, strip, :] + W * (ends + shifted(pair, j, t, 1))
+        for t, strip in every:
+            for j in range(n):
+                r0 = strip.start
+                v = wb[j, strip, :]
+                v = v + jnp.where(yi % 2 == 0, wb[j, r0 + 1 : r0 + 9, :], wb[j, r0 - 1 : r0 + 7, :])
+                v = v + jnp.where(zi % 2 == 0, roll(v, -1, 1), roll(v, 1, 1))
+                wr[j, strip, :] = (0.5 * on2[j]) * (grid[t] * v)
+        for t, strip in every:
+            for j in range(1, n - 1):
+                v = (2.0 * W - 6.0 * W * W) * wr[j, strip, :]
+                v = v + (W * W) * (wr[j - 1, strip, :] + wr[j + 1, strip, :] + shifted(wr, j, t, 2))
+                we[j, strip, :] = on2[j] * (grid[t] * v)
         k0 = (b0 + 2) * 2 - a0
-        spread = jnp.stack([e, e], axis=1).reshape(2 * e.shape[0], wy, bz)
-        d = d[k0 : k0 + spread.shape[0]]
-        v = W * d + spread
-        out = v[1:-1] + W * (d[1:-1] - (6.0 * v[1:-1] - beside(v, 1)))
-        p0 = (b0 + 2) * 2 + 1
-        return jnp.where(dims(p0, p0 + out.shape[0], 1), out, 0.0), p0
+        for t, strip in every:
+            for j in range(2, n - 2):
+                v = wr[j, strip, :] + (we[j - 1, strip, :] + we[j + 1, strip, :] + shifted(we, j, t, 2))
+                v = on2[j] * (grid[t] * ((1.0 - 6.0 * W) * we[j, strip, :] + W * v))
+                for k in (2 * j - 4, 2 * j - 3):
+                    wv[k, strip, :] = W * wd[k0 + k, strip, :] + v
+        for t, strip in every:
+            for k in range(1, 2 * n - 9):
+                v = wd[k0 + k, strip, :] + (wv[k - 1, strip, :] + wv[k + 1, strip, :] + shifted(wv, k, t, 1))
+                v = there(a0 + k0 + k, 1) * (grid[t] * ((1.0 - 6.0 * W) * wv[k, strip, :] + W * v))
+                prol[k - 1, pl.ds(16 * t, 8, stride=2), :] = v
+                prol[k - 1, pl.ds(16 * t + 1, 8, stride=2), :] = v
 
     def dot(x, m):
         out = None
@@ -432,39 +465,36 @@
         place_halo(c)
         rref = fld.at[c]
         arrive(gathered(c), rsem.at[2 * c + 1], 2)
-        e1, p0 = coarse(c)
-        e1 = e1[ex - 1 - p0 : ex + hx + 1 - p0, ey - 4 : ey + hy + 4]
-        n = hy + 8
-        prol[:, pl.ds(0, n, stride=2), :] = e1
-        prol[:, pl.ds(1, n, stride=2), :] = e1
+        coarse(c)
+        kept = slice(2 * ey - 8, 2 * ey + by + 8)
         for side, a in ((0, q - 1), (1, q + hz)):
             o = W * pk[c, side]
             for j in range(hx + 2):
-                o = o + jnp.where(lanef // 4 == j, prol[j, :, a : a + 1], 0.0)
+                o = o + jnp.where(lanef // 4 == j, prol[j, kept, a : a + 1], 0.0)
             vpk[side] = o
-        fine = dot(prol[...].reshape((hx + 2) * 2 * n, bz), grow[...]).reshape(hx + 2, 2 * n, bz)
+        fine = dot(prol[:, kept, :].reshape((hx + 2) * (by + 16), bz), grow[...]).reshape(hx + 2, by + 16, bz)
         for i in range(bx + 4):
             vfld[i] = W * rref[i] + fine[i // 2]
         for i in range(1, bx + 3):
             a, b = 7, 9 + by
-            z = vfld[i, a:b, :] + W * (rref[i, a:b, :] - operate(vfld, vpk, i, a, b))
+            z = (1.0 - 6.0 * W) * vfld[i, a:b, :] + W * (rref[i, a:b, :] + around(vfld, vpk, i, a, b))
             zrow = lax.broadcasted_iota(jnp.int32, z.shape, 0)
-            inside = ((zrow > 0) | (gy > 0)) & ((zrow < by + 1) | (gy < ny - 1))
+            ok = ((zrow > 0) | (gy > 0)) & ((zrow < by + 1) | (gy < ny - 1))
             if i == 1:
-                inside = inside & (gx > 0)
+                ok = ok & (gx > 0)
             if i == bx + 2:
-                inside = inside & (gx < nx - 1)
-            zfld[i, a:b, :] = jnp.where(inside, z, 0.0)
+                ok = ok & (gx < nx - 1)
+            zfld[i, a:b, :] = jnp.where(ok, z, 0.0)
         for side, a in ((0, 0), (1, bz - 1)):
             o = vpk[side]
             s = roll(o, 2, 1) + roll(o, -2, 1) + roll(o, 1, 0) + roll(o, -1, 0)
             s = s + roll(o, 1 - 2 * side, 1)
             for i in range(2, bx + 2):
                 s = s + jnp.where(lanef == 2 * i + 1 - side, vfld[i, :, a : a + 1], 0.0)
-            inside = gz < nz - 1 if side else gz > 0
-            zpk[side] = jnp.where(inside, o + W * (pk[c, side] - (6.0 * o - s)), 0.0)
+            ok = gz < nz - 1 if side else gz > 0
+            zpk[side] = jnp.where(ok, (1.0 - 6.0 * W) * o + W * (pk[c, side] + s), 0.0)
         z = zfld[2 : bx + 2, 8 : 8 + by, :]
-        return z, jnp.stack([operate(zfld, zpk, i, 8, 8 + by) for i in range(2, bx + 2)])
+        return z, jnp.stack([6.0 * z[i - 2] - around(zfld, zpk, i, 8, 8 + by) for i in range(2, bx + 2)])
 
     z0, w = cycle_and_image(0, r0)
     u, aw = cycle_and_image(1, w)
@@ -483,10 +513,13 @@
         ).start()
 
     if total <= 64:
-        ways = [[lax.rem(g + j, n) for j in range(n)] for g, n in zip((gx, gy, gz), ns)]
-        for j in sorted(itertools.product(*(range(n) for n in ns)), key=lambda j: -sum(min(a, n - a) for a, n in zip(j, ns))):
+        def ways(g, n):
+            return [g, g + 1 - 2 * (g % 2), lax.rem(g + 2, 4), 3 - g] if n == 4 else [lax.rem(g + j, n) for j in range(n)]
+
+        options = [ways(g, n) for g, n in zip((gx, gy, gz), ns)]
+        for j in sorted(itertools.product(*(range(n) for n in ns)), key=lambda j: -sum(j)):
             if any(j):
-                share(tuple(way[a] for way, a in zip(ways, j)))
+                share(tuple(way[i] for way, i in zip(options, j)))
     else:
 
         def step(i, carry):
@@ -512,8 +545,8 @@
     for p in range(bx):
         d1 = (z0[p] - a * u[p]) + beta * z0[p]
         i1 = (w[p] - a * aw[p]) + beta * w[p]
-        field_out[p] = a * z0[p] + b * d1
-        residual_out[p] = (r0[p] - a * w[p]) - b * i1
+        both[0, p] = a * z0[p] + b * d1
+        both[1, p] = (r0[p] - a * w[p]) - b * i1
     arrive([item for c in (0, 1) for item in halo(c) + gathered(c)], ssem.at[0], 1, total - 1)
 
 
@@ -533,11 +566,12 @@
             return pltpu.VMEM(shape, dtype)
 
         wy = (2 * ky + 1) * hy
-        return pl.pallas_call(
+        pairs = hx // 2 + REACH - 1
+        both = pl.pallas_call(
             functools.partial(kernel, ns, bx, by, bz, kx, ky),
-            out_shape=[vmem(bx, by, bz)] * 2,
+            out_shape=vmem(2, bx, by, bz),
             in_specs=[pl.BlockSpec(memory_space=pl.ANY)] * 4,
-            out_specs=[pl.BlockSpec(memory_space=pltpu.VMEM)] * 2,
+            out_specs=pl.BlockSpec(memory_space=pltpu.VMEM),
             scratch_shapes=[
                 vmem(2, bx + 4, by + 16, bz),
                 vmem(2, 2, 2, bx, bz),
@@ -555,9 +589,16 @@
                 vmem(2, 2, hy, bz),
                 vmem(2, (2 * kx + 1) * 4, wy, bz),
                 vmem(2, 2, 2 * kx + 1, wy, bz),
-                vmem(hx + 2, by + 16, bz),
+                vmem(hx + 2, 2 * wy, bz),
                 vmem(total, 1, bz),
                 vmem(ROWS, 1, bz),
+                vmem(2 * kx + 1, wy + 16, bz),
+                vmem(hx + 2 * REACH, wy + 16, bz),
+                vmem(pairs, wy + 16, bz),
+                vmem(pairs, wy + 16, bz),
+                vmem(pairs, wy + 16, bz),
+                vmem(pairs, wy + 16, bz),
+                vmem(2 * (pairs - 4), wy + 16, bz),
                 vmem(bx + 4, by + 16, bz),
                 vmem(2, by + 16, bz),
                 vmem(bx + 4, by + 16, bz),
@@ -572,6 +613,7 @@
             ],
             compiler_params=pltpu.CompilerParams(collective_id=0, has_side_effects=True),
         )(density, x_faces, y_faces, z_faces)
+        return both[0], both[1]
 
     return jax.shard_map(
         local,

time: 24.4 us -> 23.3 us (0.955)
  local copies, waits for them, and re-layouts: 1.26 us -> 0.66 us
  Pallas kernels: 22.3 us -> 21.8 us
    unnamed x2 -> x0, local copies, waits for them, and re-layouts: 1.26 us -> none
    squeeze x0 -> x1, local copies, waits for them, and re-layouts: none -> 0.66 us  [local(): return (both[0], both[1])]
    pallas_call x1, Pallas kernels: 22.3 us -> 21.8 us  [local(): pl.pallas_call(functools.partial(kernel, ns, bx, by, bz, kx, ky), out_sha...]
where the time goes in v3:
time: 23.3 us; the launch traced here: 23.1 us
  Pallas kernels  21.8 us (94%)
  local copies, waits for them, and re-layouts  0.66 us (3%)
  between operations  0.64 us (3%)
    pallas_call x1, Pallas kernels, local(): pl.pallas_call(functools.partial(kernel, ns, bx, by, bz, kx, ky), out_sha...  21.8 us
    squeeze x1, local copies, waits for them, and re-layouts, local(): return (both[0], both[1])  0.66 us

profile of v3, /device:TPU:0, one launch (start us, length us, event | category | flops | bytes accessed | tf_op | source)
XLA Modules:
  0.0 23.1 jit_solution(12592928355365771193)
XLA Ops:
  0.6 21.8 %shard_map.59 = f32[2,8,16,128]{3,2,1,0:T(8,128)S(1)} custom-call(f32[8,16,128]{2,1,0:T(8,128)} %den_in.1, f32[2,16,128]{2,1,0:T(8,128)} %xf_in.1, f32[2,8,128]{2,1,0:T(8,128)} %yf_in.1, f32[2,8,16]{2,1,0:T(8,128)} %zf_in.1), custom_call_target="tpu_custom_call" | custom-call | tf_op jit(solution)/shard_map/pallas_call | solution.py:570
  22.4 0.7 %slice_bitcast_fusion = (f32[8,16,128]{2,1,0:T(8,128)}, f32[8,16,128]{2,1,0:T(8,128)}) fusion(f32[2,8,16,128]{3,2,1,0:T(8,128)S(1)} %shard_map.59), kind=kLoop, calls=%fused_computation | loop fusion | bytes 262144 | tf_op jit(solution)/shard_map/squeeze | solution.py:616

commit v4 on v3

--- a/solution.py
+++ b/solution.py
@@ -14,6 +14,7 @@
 REACH = 7
 CUT = 8
 CHUNK = 16
+DOWN, UP, SKIN, TILES = 4, 5, 6, 5
 ROWS = 2048
 
 
@@ -51,6 +52,10 @@
     return out
 
 
+def chunk_of(piece):
+    return piece + 2 if piece < DOWN else piece - DOWN if piece < SKIN else SKIN
+
+
 def knows_all(ns, kx, ky):
     return ns[0] - 1 <= 3 * kx and ns[1] - 1 <= 3 * ky and ns[2] - 1 <= 3
 
@@ -60,7 +65,7 @@
     den_in, xf_in, yf_in, zf_in, both,
     fld, ysrc, yrec, zsrc, zrec, xyrec, pk,
     tu, tx, ty, shrink, grow, dsrc, dside, win, wside, prol, sums, blank,
-    wedge, wd, pair, wb, wr, we, wv, vfld, vpk, zfld, zpk, den, xf, yf, zf,
+    wedge, beyond, wd, pair, wb, wr, we, wv, vfld, vpk, zfld, zpk, den, xf, yf, zf,
     ssem, rsem, isem,
 ):
     nx, ny, nz = ns
@@ -145,7 +150,7 @@
         ((lj - q + hz) % hz, lj >= 0),
         (hz - CUT + lj % CHUNK, lj % CHUNK <= CUT),
         (lj % CHUNK - 1, lj % CHUNK <= CUT),
-        (jnp.where(lj < q, -1, hz), (lj < q) | (lj >= q + hz)),
+        (jnp.where(lj % CHUNK == 1, hz, -1), (lj % CHUNK == 1) | (lj % CHUNK == CUT - 1)),
     )
     for i, (col, ok) in enumerate(maps):
         ok = ok & ((col >= 0) | (gz > 0)) & ((col < hz) | (gz < nz - 1))
@@ -233,7 +238,8 @@
             if far[2]:
                 src, dst = dside.at[c, (dz + 1) // 2], wside.at[c, (1 - dz) // 2, kx - dx, rows]
             else:
-                src, dst = dsrc.at[c], win.at[c, pl.ds((kx - dx) * 4, 4), rows]
+                a, n = ((dx + 2) // 2, 3) if far[0] == 2 else (0, 4)
+                src, dst = dsrc.at[c, pl.ds(a, n)], win.at[c, pl.ds((kx - dx) * TILES + a, n), rows]
             out.append((d, send, recv, key, far, src, dst))
         return out
 
@@ -292,19 +298,20 @@
         def piece(i, k):
             return y[8 * i : 8 * i + 8, k * bz : (k + 1) * bz]
 
-        for i in range(hx // 2 + 1):
-            dsrc[c, i] = jnp.where(center, piece(2 * i, 0), piece(2 * i + 1, 0))
-        skin = jnp.where(center, piece(hx + 2, 0), 0.0)
+        skin = piece(SKIN, 0)
         for i in range(hx):
-            skin = jnp.where((lane8 == q - 1 - 2 * i) | (lane8 == q + hz + 2 * i), piece(i, 3), skin)
-        dsrc[c, hx // 2 + 1] = skin
+            skin = jnp.where(lane8 // CHUNK == chunk_of(i), piece(i, 3), skin)
+        block = [skin] + [
+            jnp.where(center, piece(a, 0), piece(b, 0)) for a, b in ((0, DOWN), (2, 1), (UP, 3))
+        ]
+        for i, tile in enumerate(block + [skin]):
+            dsrc[c, i] = tile
+            win[c, kx * TILES + i, ky * hy : (ky + 1) * hy, :] = tile
         for s, k in ((1, 1), (0, 2)):
             out = jnp.zeros((8, bz), f32)
             for i in range(hx + 3):
-                out = jnp.where(lane8 // CHUNK == i, piece(i, k), out)
+                out = jnp.where(lane8 // CHUNK == chunk_of(i), piece(i, k), out)
             dside[c, s] = out
-        for i in range(hx // 2 + 2):
-            win[c, kx * 4 + i, ky * hy : (ky + 1) * hy, :] = dsrc[c, i]
 
     def place_halo(c):
         for p in range(bx):
@@ -345,9 +352,13 @@
     mid = (zi >= q) & (zi < q + hz)
     low, high = (zi >= q - CUT) & (zi <= q), (zi >= q + hz - 1) & (zi < q + hz + CUT)
     if nz == 2:
-        sides = [(1 - gz, jnp.where(gz == 0, q + hz - 1, q - CUT), (high & (gz == 0)) | (low & (gz == 1)))]
+        sides = [(
+            1 - gz, jnp.where(gz == 0, q + hz - 1, q - CUT), (high & (gz == 0)) | (low & (gz == 1)),
+            mid & (zi % CHUNK == jnp.where(gz == 0, 1, CUT - 1)),
+        )]
     else:
-        sides = [(0, q - CUT, low), (1, q + hz - 1, high)] if nz > 1 else []
+        sides = [(0, q - CUT, low, mid & (zi % CHUNK == CUT - 1)), (1, q + hz - 1, high, mid & (zi % CHUNK == 1))]
+        sides = sides if nz > 1 else []
     strips = [slice(8 + 8 * t, 16 + 8 * t) for t in range(wy // 8)]
 
     def grid_strip(t):
@@ -372,38 +383,49 @@
             roll(v, step, 1), roll(v, -step, 1),
         ])
 
+    def helpers(c, rows):
+        def tile(i, j):
+            return win[c, TILES * i + j, rows, :]
+
+        def along(n, i, piece):
+            return pltpu.roll(beyond[n, i, rows, :], (sides[n][1] - CHUNK * chunk_of(piece)) % bz, 1)
+
+        def over(parts):
+            return [
+                jnp.where(side[2], total_of([along(n, i, f) for i, f in parts]), 0.0)
+                for n, side in enumerate(sides)
+            ]
+
+        return tile, over
+
     def assemble(c, a0, a1):
-        def side_of(i, k, rows):
-            return [
-                (m, pltpu.roll(wside[c, s, i, rows, :], (base - CHUNK * k) % bz, 1)) for s, base, m in sides
-            ]
-
+        blocks = range(2 * kx + 1)
         for t, strip in enumerate(strips):
             rows = slice(8 * t, 8 * t + 8)
-            for i in range(2 * kx + 1):
-                e = jnp.where(mid, win[c, 4 * i + hx // 2 + 1, rows, :], 0.0)
-                for m, v in side_of(i, hx + 2, rows):
-                    e = e + jnp.where(m, v, 0.0)
-                wedge[i, strip, :] = e
+
+            tile, over = helpers(c, rows)
+            for i in blocks:
+                skin = tile(i, 4 if i == 0 else 0)
+                for n, (s, _, _, spill) in enumerate(sides):
+                    beyond[n, i, rows, :] = wside[c, s, i, rows, :] + jnp.where(spill, skin, 0.0)
+                wedge[i, strip, :] = total_of([jnp.where(mid, roll(skin, hz, 1), 0.0)] + over([(i, SKIN)]))
         for t, strip in enumerate(strips):
             rows = slice(8 * t, 8 * t + 8)
+
+            tile, over = helpers(c, rows)
             for p in range(a0, a1):
                 i, k = p // hx, p % hx
-                parts = [(i, k)]
+                body, parts = tile(i, (1, 2, 2, 3)[k]), [(i, k)]
                 if k == 0 and i > 0:
-                    parts.append((i - 1, hx + 1))
+                    body = body + tile(i - 1, 3)
+                    parts.append((i - 1, UP))
                 if k == hx - 1 and i < 2 * kx:
-                    parts.append((i + 1, hx))
-                inner_part = total_of([roll(win[c, 4 * j + f // 2, rows, :], hz * (f % 2), 1) for j, f in parts])
-                terms = [jnp.where(mid, inner_part, 0.0)]
-                found = [side_of(j, f, rows) for j, f in parts]
-                for n, (_, _, m) in enumerate(sides):
-                    terms.append(jnp.where(m, total_of([f[n][1] for f in found]), 0.0))
+                    body = body + tile(i + 1, 1)
+                    parts.append((i + 1, DOWN))
+                terms = [jnp.where(mid, roll(body, hz * (k % 2), 1), 0.0)] + over(parts)
                 up = 8 + 8 * t + k + 1
                 down = 8 + 8 * t - hx + k
                 terms.append(jnp.where(yi == 7, wedge[i, up : up + 8, :], jnp.where(yi == 0, wedge[i, down : down + 8, :], 0.0)))
-                skin = win[c, 4 * i + hx // 2 + 1, rows, :]
-                terms.append(jnp.where(zi == q - 1, roll(skin, 2 * k, 1), jnp.where(zi == q + hz, roll(skin, -2 * k, 1), 0.0)))
                 wd[p - a0, strip, :] = total_of(terms)
 
     def coarse(c):
@@ -556,7 +578,7 @@
     def local(density, x_faces, y_faces, z_faces):
         bx, by, bz = density.shape
         hx, hy = bx // 2, by // 2
-        assert hx == 4 and hy == 8
+        assert hx == 4 and hy == 8 and REACH == 7
         kx, ky = -(-REACH // hx), -(-REACH // hy)
         total = ns[0] * ns[1] * ns[2]
         f32 = jnp.float32
@@ -585,14 +607,15 @@
                 vmem(2 * hx, bz),
                 vmem(2 * bz, 4 * bz, dtype=jnp.bfloat16),
                 vmem(bz, bz, dtype=jnp.bfloat16),
-                vmem(2, 4, hy, bz),
+                vmem(2, TILES, hy, bz),
                 vmem(2, 2, hy, bz),
-                vmem(2, (2 * kx + 1) * 4, wy, bz),
+                vmem(2, (2 * kx + 1) * TILES, wy, bz),
                 vmem(2, 2, 2 * kx + 1, wy, bz),
                 vmem(hx + 2, 2 * wy, bz),
                 vmem(total, 1, bz),
                 vmem(ROWS, 1, bz),
                 vmem(2 * kx + 1, wy + 16, bz),
+                vmem(2, 2 * kx + 1, wy, bz),
                 vmem(hx + 2 * REACH, wy + 16, bz),
                 vmem(pairs, wy + 16, bz),
                 vmem(pairs, wy + 16, bz),

time: 23.3 us -> 22.6 us (0.970)
  Pallas kernels: 21.8 us -> 21.1 us
    pallas_call x1, Pallas kernels: 21.8 us -> 21.1 us  [local(): pl.pallas_call(functools.partial(kernel, ns, bx, by, bz, kx, ky), out_sha...]
where the time goes in v4:
time: 22.6 us; the launch traced here: 22.4 us
  Pallas kernels  21.1 us (93%)
  local copies, waits for them, and re-layouts  0.66 us (3%)
  between operations  0.64 us (3%)
    pallas_call x1, Pallas kernels, local(): pl.pallas_call(functools.partial(kernel, ns, bx, by, bz, kx, ky), out_sha...  21.1 us
    squeeze x1, local copies, waits for them, and re-layouts, local(): return (both[0], both[1])  0.66 us

profile of v4, /device:TPU:0, one launch (start us, length us, event | category | flops | bytes accessed | tf_op | source)
XLA Modules:
  0.0 22.4 jit_solution(1668216126345396260)
XLA Ops:
  0.6 21.1 %shard_map.59 = f32[2,8,16,128]{3,2,1,0:T(8,128)S(1)} custom-call(f32[8,16,128]{2,1,0:T(8,128)} %den_in.1, f32[2,16,128]{2,1,0:T(8,128)} %xf_in.1, f32[2,8,128]{2,1,0:T(8,128)} %yf_in.1, f32[2,8,16]{2,1,0:T(8,128)} %zf_in.1), custom_call_target="tpu_custom_call" | custom-call | tf_op jit(solution)/shard_map/pallas_call | solution.py:592
  21.7 0.7 %slice_bitcast_fusion = (f32[8,16,128]{2,1,0:T(8,128)}, f32[8,16,128]{2,1,0:T(8,128)}) fusion(f32[2,8,16,128]{3,2,1,0:T(8,128)S(1)} %shard_map.59), kind=kLoop, calls=%fused_computation | loop fusion | bytes 262144 | tf_op jit(solution)/shard_map/squeeze | solution.py:639

commit v5 on v4

--- a/solution.py
+++ b/solution.py
@@ -139,10 +139,10 @@
     clear(1)
     pk[...] = jnp.zeros_like(pk)
     tx[...] = jnp.zeros_like(tx)
-    for ref in (wedge, wd, pair, wb, wr, we, wv):
-        rim = jnp.zeros((ref.shape[0], 8, bz), f32)
-        ref[:, 0:8, :] = rim
-        ref[:, ref.shape[1] - 8 :, :] = rim
+    for ref, edge in ((wedge, 8), (wd, 8), (pair, 8), (wb, 8), (wr, 8), (we, 16), (wv, 16)):
+        rim = jnp.zeros((ref.shape[0], edge, bz), f32)
+        ref[:, 0:edge, :] = rim
+        ref[:, ref.shape[1] - edge :, :] = rim
 
     lj = lane_of((bz, bz))
     li = row_of((bz, bz))
@@ -158,7 +158,10 @@
         outer = ((li == 2 * col - 1) | (li == 2 * col + 2)) & ok
         shrink[0:bz, i * bz : (i + 1) * bz] = jnp.where(cell, 0.5, 0.0).astype(bf16)
         shrink[bz : 2 * bz, i * bz : (i + 1) * bz] = jnp.where(outer, 0.5, 0.0).astype(bf16)
-    grow[...] = jnp.where(li == q + lj // 2, 1.0, 0.0).astype(bf16)
+    beyond_at = [jnp.where(gz == 0, q + hz, q - 1)] if nz == 2 else [q - 1, q + hz]
+    grow[:, 0:bz] = jnp.where(li == q + lj // 2, 1.0, 0.0).astype(bf16)
+    for n, col in enumerate(beyond_at):
+        grow[:, (n + 1) * bz : (n + 2) * bz] = jnp.where(li == col, 1.0, 0.0).astype(bf16)
 
     wait_rows(sum(rows_of(a) for a in (den, xf, yf)), isem.at[0])
     loads[-1].wait()
@@ -182,7 +185,6 @@
     r0 = jnp.stack(planes)
 
     lane8 = lane_of((8, bz))
-    lanef = lane_of((by + 16, bz))
     halves = by // 8
     own = pl.ds(8, by)
 
@@ -226,7 +228,8 @@
                 src, dst = ysrc.at[c, (dy + 1) // 2, 0], xyrec.at[c, (1 - dx) + (1 - dy) // 2]
             else:
                 slot = 1 + (1 - dx) // 2 if far[0] else 3 + (1 - dy) // 2 if far[1] else 0
-                src, dst = zsrc.at[c, (dz + 1) // 2], zrec.at[c, (1 - dz) // 2, slot]
+                a, b = (0, 0) if nz == 2 else ((dz + 1) // 2, (1 - dz) // 2)
+                src, dst = zsrc.at[c, a], zrec.at[c, b, slot]
             out.append((d, send, recv, key, far, src, dst))
         return out
 
@@ -259,14 +262,15 @@
             for d in (0, 1):
                 ysrc[c, 0, d, p : p + 1, :] = value[p, d : d + 1, :]
                 ysrc[c, 1, d, p : p + 1, :] = value[p, by - 1 - d : by - d, :]
-        for side, a in ((0, 0), (1, bz - 2)):
+        for n, (a, swap) in enumerate([(jnp.where(gz == 0, bz - 2, 0), gz == 1)] if nz == 2 else [(0, True), (bz - 2, False)]):
             out = jnp.zeros((8, bz), f32)
             for h in range(halves):
                 for p in range(bx):
                     to = 2 * (h * bx + p)
-                    moved = roll(value[p, 8 * h : 8 * h + 8, :], to - a, 1)
+                    moved = pltpu.roll(value[p, 8 * h : 8 * h + 8, :], (to + bz - a) % bz, 1)
                     out = jnp.where(lane8 // 2 == to // 2, moved, out)
-            zsrc[c, side] = out
+            turned = jnp.where(lane8 % 2 == 0, roll(out, -1, 1), roll(out, 1, 1))
+            zsrc[c, n] = jnp.where(swap, turned, out)
 
     def send_coarse(c, v):
         for i in range(hx):
@@ -322,7 +326,7 @@
             plane, p = ((1, bx - 1), (bx + 2, 0))[i // 2]
             a = (7, 8 + by)[i % 2]
             fld[c, plane, a : a + 1, :] = xyrec[c, i, p : p + 1, :]
-        for side in (0, 1):
+        for side in range(len(beyond_at)):
             t = [zrec[c, side, i] for i in range(5)]
             for h in range(halves):
                 o = jnp.where((lane8 >= 4) & (lane8 < 4 + 2 * bx), roll(t[0], 4 - 2 * bx * h, 1), 0.0)
@@ -340,8 +344,12 @@
         ln = lane_of(c.shape)
         s = ref[i - 1, a:b, :] + ref[i + 1, a:b, :]
         s = s + ref[i, a - 1 : b - 1, :] + ref[i, a + 1 : b + 1, :]
-        s = s + jnp.where(ln == 0, packed[0, a:b, 2 * i + 1 : 2 * i + 2], roll(c, 1, 1))
-        return s + jnp.where(ln == bz - 1, packed[1, a:b, 2 * i : 2 * i + 1], roll(c, -1, 1))
+        near = slice(2 * i + 1, 2 * i + 2)
+        if nz == 2:
+            s = s + jnp.where(ln == 0, 0.0, roll(c, 1, 1)) + jnp.where(ln == bz - 1, 0.0, roll(c, -1, 1))
+            return s + jnp.where(ln == (1 - gz) * (bz - 1), packed[0, a:b, near], 0.0)
+        s = s + jnp.where(ln == 0, packed[0, a:b, near], roll(c, 1, 1))
+        return s + jnp.where(ln == bz - 1, packed[1, a:b, near], roll(c, -1, 1))
 
     wy = (2 * ky + 1) * hy
     ex = kx * hx
@@ -361,8 +369,10 @@
         sides = sides if nz > 1 else []
     strips = [slice(8 + 8 * t, 16 + 8 * t) for t in range(wy // 8)]
 
-    def grid_strip(t):
-        y = yi + 8 * t
+    late = [slice(8 + ey - 4 + r, 16 + ey - 4 + r) for r in range(0, hy + 8, 8)]
+
+    def grid_strip(strip):
+        y = yi + strip.start - 8
         ok = (y >= ey - gy * hy) & (y < ey + (ny - gy) * hy) & (zi >= q - gz * hz) & (zi < q + (nz - gz) * hz)
         return jnp.where(ok, 1.0, 0.0)
 
@@ -375,9 +385,9 @@
             terms = [a + b for a, b in zip(terms[::2], terms[1::2])] + ([terms[-1]] if len(terms) % 2 else [])
         return terms[0]
 
-    def shifted(ref, p, t, step):
-        v = ref[p, strips[t], :]
-        r0 = strips[t].start
+    def shifted(ref, p, strip, step):
+        v = ref[p, strip, :]
+        r0 = strip.start
         return total_of([
             ref[p, r0 - step : r0 - step + 8, :], ref[p, r0 + step : r0 + step + 8, :],
             roll(v, step, 1), roll(v, -step, 1),
@@ -434,40 +444,41 @@
         n = (a1 - a0) // 2 - 1
         b0 = (a0 + 1) // 2
         on2 = [there(b0 + j, 2) for j in range(n)]
-        grid = [grid_strip(t) for t in range(len(strips))]
-        every = list(enumerate(strips))
-        for t, strip in every:
+        for strip in strips:
             for j in range(n):
                 pair[j, strip, :] = wd[2 * j + 1, strip, :] + wd[2 * j + 2, strip, :]
-        for t, strip in every:
+        for strip in strips:
             for j in range(n):
                 ends = wd[2 * j, strip, :] + wd[2 * j + 3, strip, :]
-                wb[j, strip, :] = (1.0 - 5.0 * W) * pair[j, strip, :] + W * (ends + shifted(pair, j, t, 1))
-        for t, strip in every:
+                wb[j, strip, :] = (1.0 - 5.0 * W) * pair[j, strip, :] + W * (ends + shifted(pair, j, strip, 1))
+        for strip in strips:
+            grid = grid_strip(strip)
             for j in range(n):
                 r0 = strip.start
                 v = wb[j, strip, :]
                 v = v + jnp.where(yi % 2 == 0, wb[j, r0 + 1 : r0 + 9, :], wb[j, r0 - 1 : r0 + 7, :])
                 v = v + jnp.where(zi % 2 == 0, roll(v, -1, 1), roll(v, 1, 1))
-                wr[j, strip, :] = (0.5 * on2[j]) * (grid[t] * v)
-        for t, strip in every:
+                wr[j, strip, :] = (0.5 * on2[j]) * (grid * v)
+        grids = [grid_strip(strip) for strip in late]
+        for strip, grid in zip(late, grids):
             for j in range(1, n - 1):
                 v = (2.0 * W - 6.0 * W * W) * wr[j, strip, :]
-                v = v + (W * W) * (wr[j - 1, strip, :] + wr[j + 1, strip, :] + shifted(wr, j, t, 2))
-                we[j, strip, :] = on2[j] * (grid[t] * v)
+                v = v + (W * W) * (wr[j - 1, strip, :] + wr[j + 1, strip, :] + shifted(wr, j, strip, 2))
+                we[j, strip, :] = on2[j] * (grid * v)
         k0 = (b0 + 2) * 2 - a0
-        for t, strip in every:
+        for strip, grid in zip(late, grids):
             for j in range(2, n - 2):
-                v = wr[j, strip, :] + (we[j - 1, strip, :] + we[j + 1, strip, :] + shifted(we, j, t, 2))
-                v = on2[j] * (grid[t] * ((1.0 - 6.0 * W) * we[j, strip, :] + W * v))
+                v = wr[j, strip, :] + (we[j - 1, strip, :] + we[j + 1, strip, :] + shifted(we, j, strip, 2))
+                v = on2[j] * (grid * ((1.0 - 6.0 * W) * we[j, strip, :] + W * v))
                 for k in (2 * j - 4, 2 * j - 3):
                     wv[k, strip, :] = W * wd[k0 + k, strip, :] + v
-        for t, strip in every:
+        for strip, grid in zip(late, grids):
             for k in range(1, 2 * n - 9):
-                v = wd[k0 + k, strip, :] + (wv[k - 1, strip, :] + wv[k + 1, strip, :] + shifted(wv, k, t, 1))
-                v = there(a0 + k0 + k, 1) * (grid[t] * ((1.0 - 6.0 * W) * wv[k, strip, :] + W * v))
-                prol[k - 1, pl.ds(16 * t, 8, stride=2), :] = v
-                prol[k - 1, pl.ds(16 * t + 1, 8, stride=2), :] = v
+                v = wd[k0 + k, strip, :] + (wv[k - 1, strip, :] + wv[k + 1, strip, :] + shifted(wv, k, strip, 1))
+                v = there(a0 + k0 + k, 1) * (grid * ((1.0 - 6.0 * W) * wv[k, strip, :] + W * v))
+                to = 2 * (strip.start - late[0].start)
+                prol[k - 1, pl.ds(to, 8, stride=2), :] = v
+                prol[k - 1, pl.ds(to + 1, 8, stride=2), :] = v
 
     def dot(x, m):
         out = None
@@ -479,42 +490,51 @@
     def cycle_and_image(c, r):
         send_halo(c, r)
         if c == 0:
+            send_coarse(c, r)
             pl.semaphore_wait(barrier, callers)
-        start(halo(c), rsem.at[2 * c])
-        send_coarse(c, r)
+            start(halo(c), rsem.at[2 * c])
+        else:
+            start(halo(c), rsem.at[2 * c])
+            send_coarse(c, r)
         start(gathered(c), rsem.at[2 * c + 1])
         arrive(halo(c), rsem.at[2 * c], 2)
         place_halo(c)
         rref = fld.at[c]
         arrive(gathered(c), rsem.at[2 * c + 1], 2)
         coarse(c)
-        kept = slice(2 * ey - 8, 2 * ey + by + 8)
-        for side, a in ((0, q - 1), (1, q + hz)):
-            o = W * pk[c, side]
+        seen = slice(6, 14 + by)
+        tall = 8 + by
+        fine = dot(prol[:, seen, :].reshape((hx + 2) * tall, bz), grow[...])
+        fine = fine.reshape(hx + 2, tall, (1 + len(beyond_at)) * bz)
+        for n in range(len(beyond_at)):
+            o = W * pk[c, n, seen, :]
             for j in range(hx + 2):
-                o = o + jnp.where(lanef // 4 == j, prol[j, kept, a : a + 1], 0.0)
-            vpk[side] = o
-        fine = dot(prol[:, kept, :].reshape((hx + 2) * (by + 16), bz), grow[...]).reshape(hx + 2, by + 16, bz)
+                o = o + jnp.where(lane_of((tall, bz)) // 4 == j, fine[j, :, (n + 1) * bz : (n + 2) * bz], 0.0)
+            vpk[n, seen, :] = o
         for i in range(bx + 4):
-            vfld[i] = W * rref[i] + fine[i // 2]
+            vfld[i, seen, :] = W * rref[i, seen, :] + fine[i // 2, :, 0:bz]
         for i in range(1, bx + 3):
-            a, b = 7, 9 + by
+            a, b = (8, 8 + by) if i in (1, bx + 2) else (7, 9 + by)
             z = (1.0 - 6.0 * W) * vfld[i, a:b, :] + W * (rref[i, a:b, :] + around(vfld, vpk, i, a, b))
             zrow = lax.broadcasted_iota(jnp.int32, z.shape, 0)
-            ok = ((zrow > 0) | (gy > 0)) & ((zrow < by + 1) | (gy < ny - 1))
             if i == 1:
-                ok = ok & (gx > 0)
-            if i == bx + 2:
-                ok = ok & (gx < nx - 1)
+                ok = gx > 0
+            elif i == bx + 2:
+                ok = gx < nx - 1
+            else:
+                ok = ((zrow > 0) | (gy > 0)) & ((zrow < by + 1) | (gy < ny - 1))
             zfld[i, a:b, :] = jnp.where(ok, z, 0.0)
-        for side, a in ((0, 0), (1, bz - 1)):
-            o = vpk[side]
-            s = roll(o, 2, 1) + roll(o, -2, 1) + roll(o, 1, 0) + roll(o, -1, 0)
-            s = s + roll(o, 1 - 2 * side, 1)
+        rows = slice(8, 8 + by)
+        lane2 = lane_of((by, bz))
+        for n in range(len(beyond_at)):
+            o = vpk[n, rows, :]
+            s = roll(o, 2, 1) + roll(o, -2, 1) + roll(o, 1, 1) + vpk[n, 7 : 7 + by, :] + vpk[n, 9 : 9 + by, :]
             for i in range(2, bx + 2):
-                s = s + jnp.where(lanef == 2 * i + 1 - side, vfld[i, :, a : a + 1], 0.0)
-            ok = gz < nz - 1 if side else gz > 0
-            zpk[side] = jnp.where(ok, (1.0 - 6.0 * W) * o + W * (pk[c, side] + s), 0.0)
+                v = vfld[i, rows, :]
+                v = jnp.where(gz == 1, v, roll(v, 1, 1)) if nz == 2 else v if n == 0 else roll(v, 1, 1)
+                s = s + jnp.where(lane2 == 2 * i + 1, v[:, 0:1], 0.0)
+            z = (1.0 - 6.0 * W) * o + W * (pk[c, n, rows, :] + s)
+            zpk[n, rows, :] = z if nz == 2 else jnp.where(gz > 0 if n == 0 else gz < nz - 1, z, 0.0)
         z = zfld[2 : bx + 2, 8 : 8 + by, :]
         return z, jnp.stack([6.0 * z[i - 2] - around(zfld, zpk, i, 8, 8 + by) for i in range(2, bx + 2)])
 
@@ -564,11 +584,10 @@
     zaz = d0 - a * (wu + zv) + a * a * uv
     cross = (d0 - a * wu) + (d0 - a * zv)
     b = g1 / (zaz + beta * cross + beta * beta * d0)
+    along_z, along_u = a + b * (1.0 + beta), a * b
     for p in range(bx):
-        d1 = (z0[p] - a * u[p]) + beta * z0[p]
-        i1 = (w[p] - a * aw[p]) + beta * w[p]
-        both[0, p] = a * z0[p] + b * d1
-        both[1, p] = (r0[p] - a * w[p]) - b * i1
+        both[0, p] = along_z * z0[p] - along_u * u[p]
+        both[1, p] = r0[p] - along_z * w[p] + along_u * aw[p]
     arrive([item for c in (0, 1) for item in halo(c) + gathered(c)], ssem.at[0], 1, total - 1)
 
 
@@ -606,12 +625,12 @@
                 vmem(hx, by + 16, bz),
                 vmem(2 * hx, bz),
                 vmem(2 * bz, 4 * bz, dtype=jnp.bfloat16),
-                vmem(bz, bz, dtype=jnp.bfloat16),
+                vmem(bz, (2 if ns[2] == 2 else 3) * bz, dtype=jnp.bfloat16),
                 vmem(2, TILES, hy, bz),
                 vmem(2, 2, hy, bz),
                 vmem(2, (2 * kx + 1) * TILES, wy, bz),
                 vmem(2, 2, 2 * kx + 1, wy, bz),
-                vmem(hx + 2, 2 * wy, bz),
+                vmem(hx + 2, by + 16, bz),
                 vmem(total, 1, bz),
                 vmem(ROWS, 1, bz),
                 vmem(2 * kx + 1, wy + 16, bz),

time: 22.6 us -> 22.3 us (0.987)
  Pallas kernels: 21.1 us -> 20.8 us
    pallas_call x1, Pallas kernels: 21.1 us -> 20.8 us  [local(): pl.pallas_call(functools.partial(kernel, ns, bx, by, bz, kx, ky), out_sha...]
where the time goes in v5:
time: 22.3 us; the launch traced here: 22.1 us
  Pallas kernels  20.8 us (93%)
  local copies, waits for them, and re-layouts  0.66 us (3%)
  between operations  0.64 us (3%)
    pallas_call x1, Pallas kernels, local(): pl.pallas_call(functools.partial(kernel, ns, bx, by, bz, kx, ky), out_sha...  20.8 us
    squeeze x1, local copies, waits for them, and re-layouts, local(): return (both[0], both[1])  0.66 us

profile of v5, /device:TPU:0, one launch (start us, length us, event | category | flops | bytes accessed | tf_op | source)
XLA Modules:
  0.0 22.1 jit_solution(16866510878215845212)
XLA Ops:
  0.6 20.8 %shard_map.59 = f32[2,8,16,128]{3,2,1,0:T(8,128)S(1)} custom-call(f32[8,16,128]{2,1,0:T(8,128)} %den_in.1, f32[2,16,128]{2,1,0:T(8,128)} %xf_in.1, f32[2,8,128]{2,1,0:T(8,128)} %yf_in.1, f32[2,8,16]{2,1,0:T(8,128)} %zf_in.1), custom_call_target="tpu_custom_call" | custom-call | tf_op jit(solution)/shard_map/pallas_call | solution.py:611
  21.4 0.7 %slice_bitcast_fusion = (f32[8,16,128]{2,1,0:T(8,128)}, f32[8,16,128]{2,1,0:T(8,128)}) fusion(f32[2,8,16,128]{3,2,1,0:T(8,128)S(1)} %shard_map.59), kind=kLoop, calls=%fused_computation | loop fusion | bytes 262144 | tf_op jit(solution)/shard_map/squeeze | solution.py:658

commit v6 on v5

--- a/solution.py
+++ b/solution.py
@@ -14,7 +14,7 @@
 REACH = 7
 CUT = 8
 CHUNK = 16
-DOWN, UP, SKIN, TILES = 4, 5, 6, 5
+DOWN, UP, SKIN, TILES = 4, 5, 6, 6
 ROWS = 2048
 
 
@@ -63,7 +63,7 @@
 def kernel(
     ns, bx, by, bz, kx, ky,
     den_in, xf_in, yf_in, zf_in, both,
-    fld, ysrc, yrec, zsrc, zrec, xyrec, pk,
+    fld, ysrc, yrec, pk,
     tu, tx, ty, shrink, grow, dsrc, dside, win, wside, prol, sums, blank,
     wedge, beyond, wd, pair, wb, wr, we, wv, vfld, vpk, zfld, zpk, den, xf, yf, zf,
     ssem, rsem, isem,
@@ -90,7 +90,7 @@
         d, send, recv, key, far = zip(*o)
         if any(far):
             window.append((d, functools.reduce(both_of, send), functools.reduce(both_of, recv), key, far))
-    window.sort(key=lambda item: -sum(f > 0 for f in item[4]))
+    window.sort(key=lambda item: (-sum(f > 0 for f in item[4]), item[3][0] + item[3][1]))
 
     def at(d):
         return (gx + d[0], gy + d[1], gz + d[2])
@@ -102,7 +102,7 @@
             pl.when(cond)(do)
 
     def clear(c):
-        for ref in (fld, yrec, zrec, xyrec, win, wside):
+        for ref in (fld, yrec, win, wside):
             ref[c] = jnp.zeros(ref.shape[1:], f32)
 
     clear(0)
@@ -216,20 +216,14 @@
         f = fld.at[c]
         out = []
         for d, send, recv, key, far in window:
-            if max(far) > 1 or sum(far) > 2:
-                continue
             dx, dy, dz = d
             if far == (1, 0, 0):
                 src = f.at[pl.ds(2 + (bx - 2) * ((dx + 1) // 2), 2), own]
                 dst = f.at[pl.ds((bx + 2) * ((1 - dx) // 2), 2), own]
             elif far == (0, 1, 0):
                 src, dst = ysrc.at[c, (dy + 1) // 2], yrec.at[c, (1 - dy) // 2]
-            elif far == (1, 1, 0):
-                src, dst = ysrc.at[c, (dy + 1) // 2, 0], xyrec.at[c, (1 - dx) + (1 - dy) // 2]
             else:
-                slot = 1 + (1 - dx) // 2 if far[0] else 3 + (1 - dy) // 2 if far[1] else 0
-                a, b = (0, 0) if nz == 2 else ((dz + 1) // 2, (1 - dz) // 2)
-                src, dst = zsrc.at[c, a], zrec.at[c, b, slot]
+                continue
             out.append((d, send, recv, key, far, src, dst))
         return out
 
@@ -239,9 +233,11 @@
             dx, dy, dz = d
             rows = pl.ds(pl.multiple_of((ky - dy) * hy, 8), hy)
             if far[2]:
-                src, dst = dside.at[c, (dz + 1) // 2], wside.at[c, (1 - dz) // 2, kx - dx, rows]
+                n = 2 if far[0] + far[1] < 2 else 1
+                src = dside.at[c, (dz + 1) // 2, pl.ds(0, n)]
+                dst = wside.at[c, (1 - dz) // 2, kx - dx, ky - dy, pl.ds(0, n)]
             else:
-                a, n = ((dx + 2) // 2, 3) if far[0] == 2 else (0, 4)
+                a, n = (1 + (dx + 2) // 2, 3) if far[0] == 2 else (0, 5) if far == (1, 1, 0) else (1, 4)
                 src, dst = dsrc.at[c, pl.ds(a, n)], win.at[c, pl.ds((kx - dx) * TILES + a, n), rows]
             out.append((d, send, recv, key, far, src, dst))
         return out
@@ -255,6 +251,8 @@
         return parts
 
     center = (lane8 >= q) & (lane8 < q + hz)
+
+    corners = ((bx - 1, by - 1), (bx - 1, 0), (0, by - 1), (0, 0))
 
     def send_halo(c, value):
         fld[c, 2 : bx + 2, 8 : 8 + by, :] = value
@@ -270,7 +268,12 @@
                     moved = pltpu.roll(value[p, 8 * h : 8 * h + 8, :], (to + bz - a) % bz, 1)
                     out = jnp.where(lane8 // 2 == to // 2, moved, out)
             turned = jnp.where(lane8 % 2 == 0, roll(out, -1, 1), roll(out, 1, 1))
-            zsrc[c, n] = jnp.where(swap, turned, out)
+            out = jnp.where(swap, turned, out)
+            for side in (0, 1) if nz == 2 else (n,):
+                dside[c, side, 1] = out
+        for i, (p, r) in enumerate(corners):
+            dsrc[c, 0, i : i + 1, :] = value[p, r : r + 1, :]
+        dsrc[c, 0, 4:8, :] = jnp.zeros((4, bz), f32)
 
     def send_coarse(c, v):
         for i in range(hx):
@@ -309,25 +312,28 @@
             jnp.where(center, piece(a, 0), piece(b, 0)) for a, b in ((0, DOWN), (2, 1), (UP, 3))
         ]
         for i, tile in enumerate(block + [skin]):
-            dsrc[c, i] = tile
-            win[c, kx * TILES + i, ky * hy : (ky + 1) * hy, :] = tile
+            dsrc[c, i + 1] = tile
+            win[c, kx * TILES + i + 1, ky * hy : (ky + 1) * hy, :] = tile
         for s, k in ((1, 1), (0, 2)):
             out = jnp.zeros((8, bz), f32)
             for i in range(hx + 3):
                 out = jnp.where(lane8 // CHUNK == chunk_of(i), piece(i, k), out)
-            dside[c, s] = out
+            dside[c, s, 0] = out
 
     def place_halo(c):
         for p in range(bx):
             for d in (0, 1):
                 fld[c, p + 2, 7 - d : 8 - d, :] = yrec[c, 0, d, p : p + 1, :]
                 fld[c, p + 2, 8 + by + d : 9 + by + d, :] = yrec[c, 1, d, p : p + 1, :]
+
+    def place_edges(c):
         for i in range(4):
-            plane, p = ((1, bx - 1), (bx + 2, 0))[i // 2]
-            a = (7, 8 + by)[i % 2]
-            fld[c, plane, a : a + 1, :] = xyrec[c, i, p : p + 1, :]
+            plane, a = (1, bx + 2)[i // 2], (7, 8 + by)[i % 2]
+            x, y = kx + 2 * (i // 2) - 1, ky + 2 * (i % 2) - 1
+            fld[c, plane, a : a + 1, :] = win[c, x * TILES, y * hy + i : y * hy + i + 1, :]
         for side in range(len(beyond_at)):
-            t = [zrec[c, side, i] for i in range(5)]
+            s = 1 - gz if nz == 2 else side
+            t = [wside[c, s, kx + x, ky + y, 1] for x, y in ((0, 0), (-1, 0), (1, 0), (0, -1), (0, 1))]
             for h in range(halves):
                 o = jnp.where((lane8 >= 4) & (lane8 < 4 + 2 * bx), roll(t[0], 4 - 2 * bx * h, 1), 0.0)
                 o = jnp.where(lane8 // 2 == 1, roll(t[1], 2 - 2 * (bx * h + bx - 1), 1), o)
@@ -415,9 +421,9 @@
 
             tile, over = helpers(c, rows)
             for i in blocks:
-                skin = tile(i, 4 if i == 0 else 0)
+                skin = tile(i, 5 if i == 0 else 1)
                 for n, (s, _, _, spill) in enumerate(sides):
-                    beyond[n, i, rows, :] = wside[c, s, i, rows, :] + jnp.where(spill, skin, 0.0)
+                    beyond[n, i, rows, :] = wside[c, s, i, t, 0] + jnp.where(spill, skin, 0.0)
                 wedge[i, strip, :] = total_of([jnp.where(mid, roll(skin, hz, 1), 0.0)] + over([(i, SKIN)]))
         for t, strip in enumerate(strips):
             rows = slice(8 * t, 8 * t + 8)
@@ -425,12 +431,12 @@
             tile, over = helpers(c, rows)
             for p in range(a0, a1):
                 i, k = p // hx, p % hx
-                body, parts = tile(i, (1, 2, 2, 3)[k]), [(i, k)]
+                body, parts = tile(i, (2, 3, 3, 4)[k]), [(i, k)]
                 if k == 0 and i > 0:
-                    body = body + tile(i - 1, 3)
+                    body = body + tile(i - 1, 4)
                     parts.append((i - 1, UP))
                 if k == hx - 1 and i < 2 * kx:
-                    body = body + tile(i + 1, 1)
+                    body = body + tile(i + 1, 2)
                     parts.append((i + 1, DOWN))
                 terms = [jnp.where(mid, roll(body, hz * (k % 2), 1), 0.0)] + over(parts)
                 up = 8 + 8 * t + k + 1
@@ -492,15 +498,17 @@
         if c == 0:
             send_coarse(c, r)
             pl.semaphore_wait(barrier, callers)
-            start(halo(c), rsem.at[2 * c])
         else:
-            start(halo(c), rsem.at[2 * c])
             send_coarse(c, r)
-        start(gathered(c), rsem.at[2 * c + 1])
+        items = gathered(c)
+        start([m for m in items if all(m[4])], rsem.at[2 * c + 1])
+        start(halo(c), rsem.at[2 * c])
+        start([m for m in items if not all(m[4])], rsem.at[2 * c + 1])
         arrive(halo(c), rsem.at[2 * c], 2)
         place_halo(c)
         rref = fld.at[c]
         arrive(gathered(c), rsem.at[2 * c + 1], 2)
+        place_edges(c)
         coarse(c)
         seen = slice(6, 14 + by)
         tall = 8 + by
@@ -617,9 +625,6 @@
                 vmem(2, bx + 4, by + 16, bz),
                 vmem(2, 2, 2, bx, bz),
                 vmem(2, 2, 2, bx, bz),
-                vmem(2, 2, 8, bz),
-                vmem(2, 2, 5, 8, bz),
-                vmem(2, 4, bx, bz),
                 vmem(2, 2, by + 16, bz),
                 vmem(hx + 2, by, bz),
                 vmem(hx, by + 16, bz),
@@ -627,9 +632,9 @@
                 vmem(2 * bz, 4 * bz, dtype=jnp.bfloat16),
                 vmem(bz, (2 if ns[2] == 2 else 3) * bz, dtype=jnp.bfloat16),
                 vmem(2, TILES, hy, bz),
-                vmem(2, 2, hy, bz),
+                vmem(2, 2, 2, hy, bz),
                 vmem(2, (2 * kx + 1) * TILES, wy, bz),
-                vmem(2, 2, 2 * kx + 1, wy, bz),
+                vmem(2, 2, 2 * kx + 1, 2 * ky + 1, 2, hy, bz),
                 vmem(hx + 2, by + 16, bz),
                 vmem(total, 1, bz),
                 vmem(ROWS, 1, bz),

time: 22.3 us -> 22.1 us (level)
  no operation moved by 1% of the time
where the time goes in v6:
time: 22.1 us; the launch traced here: 21.9 us
  Pallas kernels  20.6 us (93%)
  local copies, waits for them, and re-layouts  0.66 us (3%)
  between operations  0.64 us (3%)
    pallas_call x1, Pallas kernels, local(): pl.pallas_call(functools.partial(kernel, ns, bx, by, bz, kx, ky), out_sha...  20.6 us
    squeeze x1, local copies, waits for them, and re-layouts, local(): return (both[0], both[1])  0.66 us

profile of v6, /device:TPU:0, one launch (start us, length us, event | category | flops | bytes accessed | tf_op | source)
XLA Modules:
  0.0 21.9 jit_solution(14692192945317030320)
XLA Ops:
  0.6 20.6 %shard_map.59 = f32[2,8,16,128]{3,2,1,0:T(8,128)S(1)} custom-call(f32[8,16,128]{2,1,0:T(8,128)} %den_in.1, f32[2,16,128]{2,1,0:T(8,128)} %xf_in.1, f32[2,8,128]{2,1,0:T(8,128)} %yf_in.1, f32[2,8,16]{2,1,0:T(8,128)} %zf_in.1), custom_call_target="tpu_custom_call" | custom-call | tf_op jit(solution)/shard_map/pallas_call | solution.py:619
  21.3 0.7 %slice_bitcast_fusion = (f32[8,16,128]{2,1,0:T(8,128)}, f32[8,16,128]{2,1,0:T(8,128)}) fusion(f32[2,8,16,128]{3,2,1,0:T(8,128)S(1)} %shard_map.59), kind=kLoop, calls=%fused_computation | loop fusion | bytes 262144 | tf_op jit(solution)/shard_map/squeeze | solution.py:663

commit v7 on v6

--- a/solution.py
+++ b/solution.py
@@ -501,13 +501,12 @@
         else:
             send_coarse(c, r)
         items = gathered(c)
-        start([m for m in items if all(m[4])], rsem.at[2 * c + 1])
-        start(halo(c), rsem.at[2 * c])
-        start([m for m in items if not all(m[4])], rsem.at[2 * c + 1])
-        arrive(halo(c), rsem.at[2 * c], 2)
+        start([m for m in items if all(m[4])], rsem.at[c])
+        start(halo(c), rsem.at[c])
+        start([m for m in items if not all(m[4])], rsem.at[c])
+        rref = fld.at[c]
+        arrive(halo(c) + gathered(c), rsem.at[c], 2)
         place_halo(c)
-        rref = fld.at[c]
-        arrive(gathered(c), rsem.at[2 * c + 1], 2)
         place_edges(c)
         coarse(c)
         seen = slice(6, 14 + by)
@@ -549,7 +548,7 @@
     z0, w = cycle_and_image(0, r0)
     u, aw = cycle_and_image(1, w)
 
-    pairs = ((r0, z0), (z0, w), (r0, u), (w, u), (u, aw), (z0, aw))
+    pairs = ((r0, z0), (z0, w), (w, u), (u, aw))
     l1 = lane_of((1, bz))
     mine = jnp.zeros((1, bz), f32)
     for i, (a, b) in enumerate(pairs):
@@ -559,7 +558,7 @@
 
     def share(to):
         pltpu.make_async_remote_copy(
-            sums.at[me], sums.at[me], ssem.at[0], rsem.at[4], device_id=to, device_id_type=MESH
+            sums.at[me], sums.at[me], ssem.at[0], rsem.at[2], device_id=to, device_id_type=MESH
         ).start()
 
     if total <= 64:
@@ -579,18 +578,18 @@
 
         lax.fori_loop(1, total, step, 0)
 
-    wait_rows(total - 1, rsem.at[4])
+    wait_rows(total - 1, rsem.at[2])
     tot = jnp.sum(sums[...], axis=0)
 
     def scalar(i):
         return jnp.sum(jnp.where(l1 == i, tot, 0.0), axis=1, keepdims=True)
 
-    g0, d0, ru, wu, uv, zv = (scalar(i) for i in range(6))
+    g0, d0, wu, uv = (scalar(i) for i in range(4))
     a = g0 / d0
-    g1 = (g0 - a * d0) - a * ru + a * a * wu
+    g1 = (g0 - a * d0) - a * d0 + a * a * wu
     beta = g1 / g0
-    zaz = d0 - a * (wu + zv) + a * a * uv
-    cross = (d0 - a * wu) + (d0 - a * zv)
+    zaz = d0 - 2.0 * a * wu + a * a * uv
+    cross = 2.0 * (d0 - a * wu)
     b = g1 / (zaz + beta * cross + beta * beta * d0)
     along_z, along_u = a + b * (1.0 + beta), a * b
     for p in range(bx):
@@ -655,7 +654,7 @@
                 vmem(*y_faces.shape),
                 vmem(*z_faces.shape),
                 dma((1,)),
-                dma((5,)),
+                dma((3,)),
                 dma((2,)),
             ],
             compiler_params=pltpu.CompilerParams(collective_id=0, has_side_effects=True),

time: 22.1 us -> 22.1 us (level)
  no operation moved by 1% of the time
where the time goes in v7:
time: 22.1 us; the launch traced here: 21.9 us
  Pallas kernels  20.6 us (93%)
  local copies, waits for them, and re-layouts  0.66 us (3%)
  between operations  0.64 us (3%)
    pallas_call x1, Pallas kernels, local(): pl.pallas_call(functools.partial(kernel, ns, bx, by, bz, kx, ky), out_sha...  20.6 us
    squeeze x1, local copies, waits for them, and re-layouts, local(): return (both[0], both[1])  0.66 us

profile of v7, /device:TPU:0, one launch (start us, length us, event | category | flops | bytes accessed | tf_op | source)
XLA Modules:
  0.0 21.9 jit_solution(10546957782725434038)
XLA Ops:
  0.6 20.6 %shard_map.59 = f32[2,8,16,128]{3,2,1,0:T(8,128)S(1)} custom-call(f32[8,16,128]{2,1,0:T(8,128)} %den_in.1, f32[2,16,128]{2,1,0:T(8,128)} %xf_in.1, f32[2,8,128]{2,1,0:T(8,128)} %yf_in.1, f32[2,8,16]{2,1,0:T(8,128)} %zf_in.1), custom_call_target="tpu_custom_call" | custom-call | tf_op jit(solution)/shard_map/pallas_call | solution.py:618
  21.3 0.7 %slice_bitcast_fusion = (f32[8,16,128]{2,1,0:T(8,128)}, f32[8,16,128]{2,1,0:T(8,128)}) fusion(f32[2,8,16,128]{3,2,1,0:T(8,128)S(1)} %shard_map.59), kind=kLoop, calls=%fused_computation | loop fusion | bytes 262144 | tf_op jit(solution)/shard_map/squeeze | solution.py:662
